TPU v7x, 32 devices: a whole 2x2x4 slice. The times are simulated.
32 devices in a mesh: groups: 2 (over y), grid: 4 (over z), depth: 4 (over x, core).
Axes of the slice: x: 2, y: 2, z: 4, core: 2. Of those that a mesh axis runs over, the one named last changes fastest.
Arguments:
- tokens: bfloat16 [512, 4096], P(('groups', 'grid'), 'depth'), parts along dimension 0, may hold values from -6 to 6
- gate_weight: bfloat16 [4096, 14336], P('depth', 'grid'), may hold values from -0.09375 to 0.09375
- up_weight: bfloat16 [4096, 14336], P('depth', 'grid'), may hold values from -0.09375 to 0.09375
- down_weight: bfloat16 [14336, 4096], P('grid', 'depth'), may hold values from -0.046875 to 0.046875
Outputs:
- mixed: bfloat16 [512, 4096], P(('groups', 'grid'), 'depth'), parts along dimension 0
There are 2 independent parts, one for each index of `groups`. A program takes and returns all parts, laid end to end along the dimension named above; an argument that names none is the same for every part. Nothing has to cross between parts.
All inputs are finite; a program needn't handle non-finite values.
Results may differ from a plain program's by a relative error of at most 0.0049.
Values may be sent and summed in bfloat16 or wider, within the bound.
No kernel may reach another device: no remote copies, remote signals or barrier semaphores. Data moves between devices by JAX's collectives and lax.ppermute only.
A program may use at most 64 MiB of HBM per device.

v0:
```python
import jax
import jax.numpy as jnp
from jax import lax
from jax.sharding import PartitionSpec as P


def body(tokens, gate_weight, up_weight, down_weight):
    grid_size = lax.axis_size("grid")
    block_rows = tokens.shape[0]
    total_rows = block_rows * grid_size
    width_share = gate_weight.shape[1]
    stacked = jnp.concatenate([gate_weight, up_weight], axis=1)
    pre_act = jnp.dot(
        lax.all_gather(tokens, "grid", axis=0, tiled=True),
        stacked,
        preferred_element_type=jnp.float32,
    )
    blocked = pre_act.reshape(grid_size, block_rows, 2 * width_share)
    summed = lax.psum_scatter(blocked, "depth", scatter_dimension=1, tiled=True)
    hidden = lax.all_gather(
        (jax.nn.silu(summed[..., :width_share]) * summed[..., width_share:]).astype(jnp.bfloat16),
        "depth",
        axis=1,
        tiled=True,
    ).reshape(total_rows, width_share)
    return lax.psum_scatter(
        jnp.dot(hidden, down_weight, preferred_element_type=jnp.float32),
        "grid",
        scatter_dimension=0,
        tiled=True,
    ).astype(jnp.bfloat16)


def solution(mesh):
    placed = (
        P(("groups", "grid"), "depth"),
        P("depth", "grid"),
        P("depth", "grid"),
        P("grid", "depth"),
    )
    return jax.shard_map(
        body, mesh=mesh, in_specs=placed, out_specs=P(("groups", "grid"), "depth"), check_vma=False
    )
```

profile of v0, /device:TPU:0, one launch (start us, length us, event | category | flops | bytes accessed | tf_op | source)
XLA Modules:
  0.0 169.0 jit_solution(2608412261926254104)
XLA Ops:
  6.5 0.0 reduce-scatter.3.cloned.1.call-start
  6.5 17.6 %all_gather.6 = bf16[256,1024]{1,0:T(8,128)(2,1)S(1)} all-gather(bf16[64,1024]{1,0:T(8,128)(2,1)} %param.4), channel_id=1, replica_groups=mesh['groups'=2,'grid'=4,'depth'=4] {'grid'}, dimensions={0}, use_global_device_ids=true | all-gather | bytes 655360 | tf_op jit(solution)/shard_map/all_gather | solution.py:14
  24.1 12.1 %fusion = f32[7168,256]{0,1:T(8,128)} fusion(bf16[256,1024]{1,0:T(8,128)(2,1)S(1)} %all_gather.6, bf16[1024,3584]{1,0:T(8,128)(2,1)} %param.6, bf16[1024,3584]{1,0:T(8,128)(2,1)} %param.5), kind=kOutput, calls=%fused_computation | convolution fusion | flops 3787456512 | bytes 22544384 | tf_op jit(solution)/shard_map/dot_general | solution.py:13
  36.2 0.0 reduce-scatter.3.cloned.1.call-update
  36.2 0.0 all-gather.2.cloned.1.call-start
  36.3 66.6 %reduce-scatter.3.cloned.1.call-done = f32[4,16,7168]{2,1,0:T(8,128)} async-done(((f32[4,64,7168]{2,1,0:T(8,128)}), f32[4,16,7168]{2,1,0:T(8,128)}) %reduce-scatter.3.cloned.1.call-update) | async-done | bytes 1835024 | tf_op jit(solution)/shard_map/reduce_scatter | solution.py:19
  102.9 2.5 %fusion.4 = bf16[4,16,3584]{2,1,0:T(8,128)(2,1)} fusion(f32[4,16,7168]{2,1,0:T(8,128)} %reduce-scatter.3.cloned.1.call-done), kind=kLoop, calls=%fused_computation.5 | loop fusion | flops 1376256 | bytes 2293760 | tf_op jit(solution)/shard_map/convert_element_type | solution.py:21
  105.4 0.0 all-gather.2.cloned.1.call-update
  105.4 0.0 reduce-scatter.5.cloned.1.call-start
  105.4 21.2 %all-gather.2.cloned.1.call-done = bf16[4,64,3584]{2,1,0:T(8,128)(2,1)} async-done(((bf16[4,16,3584]{2,1,0:T(8,128)(2,1)}), bf16[4,64,3584]{2,1,0:T(8,128)(2,1)}) %all-gather.2.cloned.1.call-update) | async-done | bytes 1835024 | tf_op jit(solution)/shard_map/all_gather | solution.py:20
  126.6 6.7 %fusion.6 = f32[256,1024]{1,0:T(8,128)} fusion(bf16[256,3584]{1,0:T(8,128)(2,1)} %bitcast.8, bf16[3584,1024]{1,0:T(8,128)(2,1)} %param.7), kind=kOutput, calls=%fused_computation.7 | convolution fusion | flops 1879048192 | bytes 10223616 | tf_op jit(solution)/shard_map/dot_general | solution.py:27
  133.3 0.0 reduce-scatter.5.cloned.1.call-update
  133.4 27.4 %reduce-scatter.5.cloned.1.call-done = f32[64,1024]{1,0:T(8,128)} async-done(((f32[256,1024]{1,0:T(8,128)}), f32[64,1024]{1,0:T(8,128)}) %reduce-scatter.5.cloned.1.call-update) | async-done | bytes 262160 | tf_op jit(solution)/shard_map/reduce_scatter | solution.py:26
  160.8 1.6 convert_element_type.7
Async XLA Ops:
  6.5 96.3 %reduce-scatter.3.cloned.1.call-start = ((), (), s32[]{:S(2)}) async-start(), calls=%async_computation.2 | async-start | bytes 9175040 | tf_op jit(solution)/shard_map/reduce_scatter | solution.py:19
  36.2 90.4 %all-gather.2.cloned.1.call-start = ((), (), s32[]{:S(2)}) async-start(), calls=%async_computation.3 | async-start | bytes 2293760 | tf_op jit(solution)/shard_map/all_gather | solution.py:20
  105.4 55.4 %reduce-scatter.5.cloned.1.call-start = ((), (), s32[]{:S(2)}) async-start(), calls=%async_computation.4 | async-start | bytes 1310720 | tf_op jit(solution)/shard_map/reduce_scatter | solution.py:26
Sparse Core Ops, SparseCore 0:
  36.4 66.4 reduce-scatter.2
  105.5 21.0 all-gather.1
  133.5 27.2 reduce-scatter.4
where the time goes:
time: 169 us
  waiting for transfers between devices  115 us (68%)
  matrix products  18.8 us (11%)
  blocking collectives  17.6 us (10%)
  between operations  13.1 us (8%)
  other arithmetic  4.12 us (2%)
    reduce_scatter x1, waiting for transfers between devices, body(): summed = lax.psum_scatter(blocked, 'depth', scatter_dimension=1, tiled=True)  66.6 us
    reduce_scatter x1, waiting for transfers between devices, body(): lax.psum_scatter(jnp.dot(hidden, down_weight, preferred_element_type=jnp....  27.4 us
    all_gather x1, waiting for transfers between devices, body(): lax.all_gather((jax.nn.silu(summed[..., :width_share]) * summed[..., widt...  21.2 us
    all_gather x1, blocking collectives, body(): lax.all_gather(tokens, 'grid', axis=0, tiled=True)  17.6 us
    dot_general x1, matrix products, body(): jnp.dot(lax.all_gather(tokens, 'grid', axis=0, tiled=True), stacked, pref...  12.1 us
    dot_general x1, matrix products, body(): jnp.dot(hidden, down_weight, preferred_element_type=jnp.float32)  6.69 us
  transfers between devices with their start and end apart: 3, of which 3 were waited for; matrix products, arithmetic and copies ran while one was open for 0% of the time, Pallas kernels for 0%

commit v1 on v0

v1 whole, which is shorter than its diff:
```python
import functools

import jax
import jax.numpy as jnp
from jax import lax
from jax.experimental import pallas as pl
from jax.experimental.pallas import tpu as pltpu
from jax.sharding import PartitionSpec as P


CHUNKS = ((0,), (1,), (3,), (2,))
ORDER = (3, 1, 2, 0)
MIB = 1024 * 1024
VMEM = pl.BlockSpec(memory_space=pltpu.VMEM)
SMEM = pl.BlockSpec(memory_space=pltpu.SMEM)


def flip(value, axis, bits):
    size = lax.axis_size(axis)
    return lax.ppermute(value, axis, [(i, i ^ bits) for i in range(size)])


def held(value):
    return pltpu.with_memory_space_constraint(value, pltpu.VMEM)


def width_of(hidden):
    return next((w for w in (896, 512, 384, 256, 128) if hidden % w == 0), hidden)


def sort_rows(me, x_refs, x_sc):
    blocks, part = len(x_refs), x_refs[0].shape[0] // len(ORDER)
    for i, r in enumerate(ORDER):
        at = pl.multiple_of((me ^ r) * part, part)
        for b in range(blocks):
            x_sc[(i * blocks + b) * part : (i * blocks + b + 1) * part, :] = x_refs[b][pl.ds(at, part), :]


def sort_kernel(me_ref, *refs):
    sort_rows(me_ref[0], refs[:-1], refs[-1])


def sort(me, xs):
    block_rows, depth = xs[0].shape
    return pl.pallas_call(
        sort_kernel,
        in_specs=[SMEM] + [VMEM] * len(xs),
        out_specs=VMEM,
        out_shape=jax.ShapeDtypeStruct((block_rows * len(xs), depth), xs[0].dtype),
        compiler_params=pltpu.CompilerParams(vmem_limit_bytes=12 * MIB),
        cost_estimate=pl.CostEstimate(flops=10**10, bytes_accessed=0, transcendentals=0),
        name="sort",
    )(me, *xs)


def up_gate_kernel(me_ref, *refs, blocks):
    x_refs, (g_ref, u_ref, send_ref, keep_ref, *scratch) = refs[:blocks], refs[blocks:]
    if scratch:
        sort_rows(me_ref[0], x_refs, scratch[0])
    x = (scratch or x_refs)[0][...]
    half = x.shape[0] // 2
    hidden = g_ref.shape[1]
    width = width_of(hidden)
    for j in range(hidden // width):
        cols = slice(j * width, (j + 1) * width)
        for i, w_ref in enumerate((g_ref, u_ref)):
            y = jnp.dot(x, w_ref[:, cols], preferred_element_type=jnp.float32)
            send_ref[i, :, cols] = y[:half].astype(send_ref.dtype)
            keep_ref[i, :, cols] = y[half:]


def up_gate(me, xs, gate, up, ordered):
    depth, hidden = gate.shape
    rows = xs[0].shape[0] * len(xs)
    return pl.pallas_call(
        functools.partial(up_gate_kernel, blocks=len(xs)),
        in_specs=[SMEM] + [VMEM] * (len(xs) + 2),
        out_specs=[VMEM] * 2,
        out_shape=[
            jax.ShapeDtypeStruct((2, rows // 2, hidden), jnp.bfloat16),
            jax.ShapeDtypeStruct((2, rows // 2, hidden), jnp.float32),
        ],
        scratch_shapes=[] if ordered else [pltpu.VMEM((rows, depth), jnp.bfloat16)],
        compiler_params=pltpu.CompilerParams(vmem_limit_bytes=12 * MIB),
        cost_estimate=pl.CostEstimate(
            flops=4 * rows * depth * hidden, bytes_accessed=4 * depth * hidden, transcendentals=0
        ),
        name="up_gate",
    )(me, *xs, held(gate), held(up))


def down_kernel(me_ref, h0, h2, h1, h3, w_ref, *outs):
    me = me_ref[0]
    h = jnp.concatenate([h0[...], h2[...], h1[...], h3[...]], axis=0)
    part = outs[0].shape[0] // len(ORDER)
    depth = w_ref.shape[1]
    width = 256 if depth % 256 == 0 else depth
    for c in range(depth // width):
        cols = slice(c * width, (c + 1) * width)
        y = jnp.dot(h, w_ref[:, cols], preferred_element_type=jnp.float32)
        for i, r in enumerate((0, 2, 1, 3)):
            at = pl.multiple_of((me ^ r) * part, part)
            for b, out in enumerate(outs):
                first = (i * len(outs) + b) * part
                out[pl.ds(at, part), cols] = y[first : first + part].astype(out.dtype)


def down(me, hs, weight, block_rows, kinds):
    hidden, depth = weight.shape
    rows = block_rows * len(kinds)
    return pl.pallas_call(
        down_kernel,
        in_specs=[SMEM] + [VMEM] * 5,
        out_specs=[VMEM] * len(kinds),
        out_shape=[jax.ShapeDtypeStruct((block_rows, depth), kind) for kind in kinds],
        compiler_params=pltpu.CompilerParams(vmem_limit_bytes=12 * MIB),
        cost_estimate=pl.CostEstimate(
            flops=2 * rows * depth * hidden, bytes_accessed=2 * depth * hidden, transcendentals=0
        ),
        name="down",
    )(me, *hs, held(weight))


def steps(tokens, gate_weight, up_weight, down_weight):
    grid_size = lax.axis_size("grid")
    block_rows = tokens.shape[0]
    me = lax.axis_index("depth").astype(jnp.int32).reshape(1)
    per = grid_size // sum(map(len, CHUNKS))
    chunks = [[s for q in chunk for s in range(q * per, (q + 1) * per)] for chunk in CHUNKS]
    blocks = {0: tokens}
    for chunk in chunks:
        for s in chunk:
            if s:
                blocks[s] = flip(tokens, "grid", s)
    total = None
    arrived = []
    for number, chunk in enumerate(chunks):
        xs = [blocks[s] for s in chunk]
        if number == 0:
            xs = [sort(me, xs)]
        send, keep = up_gate(me, xs, gate_weight, up_weight, number == 0)
        part = keep.shape[1] // 2
        recv = flip(send, "depth", 1)
        across = (keep[:, :part] + recv[:, :part].astype(jnp.float32)).astype(jnp.bfloat16)
        crossed = flip(across, "depth", 2)
        both = keep[:, part:] + recv[:, part:].astype(jnp.float32) + crossed.astype(jnp.float32)
        mine = (jax.nn.silu(both[0]) * both[1]).astype(jnp.bfloat16)
        other = flip(mine, "depth", 2)
        mine_passed = flip(mine, "depth", 1)
        other_passed = flip(other, "depth", 1)
        kinds = [jnp.bfloat16 if s else jnp.float32 for s in chunk]
        outs = down(me, (mine, other, mine_passed, other_passed), down_weight, block_rows, kinds)
        for s, out in zip(chunk, outs):
            if s:
                arrived.append(flip(out, "grid", s))
            else:
                total = out
    for value in arrived:
        total = total + value.astype(jnp.float32)
    return total.astype(jnp.bfloat16)


def solution(mesh):
    placed = (
        P(("groups", "grid"), "depth"),
        P("depth", "grid"),
        P("depth", "grid"),
        P("grid", "depth"),
    )
    return jax.shard_map(
        steps, mesh=mesh, in_specs=placed, out_specs=P(("groups", "grid"), "depth"), check_vma=False
    )
```

time: 169 us -> 79.7 us (0.47)
  waiting for transfers between devices: 115 us -> 33.1 us
  starting transfers between devices: 0.09 us -> 23 us
  matrix products: 18.8 us -> 0 us
  blocking collectives: 17.6 us -> 0 us
  Pallas kernels: 0 us -> 15.8 us
  between operations: 13.1 us -> 0.23 us
  local copies, waits for them, and re-layouts: 0 us -> 6.07 us
  other arithmetic: 4.12 us -> 1.42 us
    reduce_scatter x2 -> x0, waiting for transfers between devices: 94 us -> none  [the longest x1 66.6 us: body(): summed = lax.psum_scatter(blocked, 'depth', scatter_dimension=1, tiled=True)]
    ppermute x0 -> x26, waiting for transfers between devices: none -> 33.1 us  [flip(): return lax.ppermute(value, axis, [(i, i ^ bits) for i in range(size)])]
    ppermute x0 -> x26, starting transfers between devices: none -> 23 us  [flip(): return lax.ppermute(value, axis, [(i, i ^ bits) for i in range(size)])]
    all_gather x1 -> x0, waiting for transfers between devices: 21.2 us -> none  [body(): lax.all_gather((jax.nn.silu(summed[..., :width_share]) * summed[..., widt...]
    dot_general x2 -> x0, matrix products: 18.8 us -> none  [the longest x1 12.1 us: body(): jnp.dot(lax.all_gather(tokens, 'grid', axis=0, tiled=True), stacked, pref...]
    all_gather x1 -> x0, blocking collectives: 17.6 us -> none  [body(): lax.all_gather(tokens, 'grid', axis=0, tiled=True)]
    pallas_call x0 -> x9, Pallas kernels: none -> 15.8 us  [the longest x4 10.3 us: up_gate(): pl.pallas_call(functools.partial(up_gate_kernel, blocks=len(xs)), in_spec...]
    unnamed x0 -> x10, local copies, waits for them, and re-layouts: none -> 6.07 us
  transfers between devices with their start and end apart: 3 -> 26, of which waited for: 3 -> 10; matrix products, arithmetic and copies ran while one was open for 0% -> 1% of each run, Pallas kernels for 0% -> 17%
where the time goes in v1:
time: 79.7 us; the launch traced here: 79.6 us
  waiting for transfers between devices  33.1 us (42%)
  starting transfers between devices  23 us (29%)
  Pallas kernels  15.8 us (20%)
  local copies, waits for them, and re-layouts  6.07 us (8%)
  other arithmetic  1.42 us (2%)
    ppermute x26, waiting for transfers between devices, flip(): return lax.ppermute(value, axis, [(i, i ^ bits) for i in range(size)])  33.1 us
    ppermute x26, starting transfers between devices, flip(): return lax.ppermute(value, axis, [(i, i ^ bits) for i in range(size)])  23 us
    pallas_call x4, Pallas kernels, up_gate(): pl.pallas_call(functools.partial(up_gate_kernel, blocks=len(xs)), in_spec...  10.3 us
    unnamed x10, local copies, waits for them, and re-layouts  6.07 us
    pallas_call x4, Pallas kernels, down(): pl.pallas_call(down_kernel, in_specs=[SMEM] + [VMEM] * 5, out_specs=[VMEM...  5.51 us
  transfers between devices with their start and end apart: 26, of which 10 were waited for; matrix products, arithmetic and copies ran while one was open for 1% of the time, Pallas kernels for 17%

profile of v1, /device:TPU:0, one launch (start us, length us, event | category | flops | bytes accessed | tf_op | source)
XLA Modules:
  0.0 79.6 jit_solution(8465154211516895136)
XLA Ops:
  0.0 0.9 %copy-done.2 = bf16[64,1024]{1,0:T(8,128)(2,1)S(1)} copy-done((bf16[64,1024]{1,0:T(8,128)(2,1)S(1)}, bf16[64,1024]{1,0:T(8,128)(2,1)}, u32[]{:S(2)}) %copy-start.2) | copy-done | bytes 131096
  0.9 3.1 %copy-done = bf16[1024,3584]{1,0:T(8,128)(2,1)S(1)} copy-done((bf16[1024,3584]{1,0:T(8,128)(2,1)S(1)}, bf16[1024,3584]{1,0:T(8,128)(2,1)}, u32[]{:S(2)}) %copy-start) | copy-done | bytes 7340056
  4.0 2.1 %copy-done.1 = bf16[1024,3584]{1,0:T(8,128)(2,1)S(1)} copy-done((bf16[1024,3584]{1,0:T(8,128)(2,1)S(1)}, bf16[1024,3584]{1,0:T(8,128)(2,1)}, u32[]{:S(2)}) %copy-start.1) | copy-done | bytes 7340056
  6.1 2.6 %up_gate.4 = (bf16[2,32,3584]{2,1,0:T(8,128)(2,1)S(1)}, f32[2,32,3584]{2,1,0:T(8,128)S(1)}) custom-call(s32[1]{0:T(128)} %bitcast.me_ref, bf16[64,1024]{1,0:T(8,128)(2,1)S(1)} %sort.1.refs_0_, bf16[1024,3584]{1,0:T(8,128)(2,1)S(1)} %copy-done, bf16[1024,3584]{1,0:T(8,128)(2,1)S(1)} %copy-done.1), custom_call_target="tpu_custom_call" | custom-call | flops 939524096 | bytes 14680064 | tf_op jit(solution)/shard_map/up_gate/pallas_call | solution.py:75
  9.2 4.7 %collective-permute-start.12 = (bf16[64,1024]{1,0:T(8,128)(2,1)S(1)}, bf16[64,1024]{1,0:T(8,128)(2,1)S(1)}, u32[]{:S(2)}, u32[]{:S(2)}) collective-permute-start(bf16[64,1024]{1,0:T(8,128)(2,1)S(1)} %copy-done.2), channel_id=1, source_target_pairs={{0,12},{4,8},{8,4},{12,0},{1,13},{5,9},{9,5},{13,1},{2,14},{6,10},... | collective-permute-start | bytes 393224 | tf_op jit(solution)/shard_map/ppermute | solution.py:20
  13.9 0.6 collective-permute-start.5
  14.5 3.8 %collective-permute-done.12.refs_0_ = bf16[64,1024]{1,0:T(8,128)(2,1)S(1)} collective-permute-done((bf16[64,1024]{1,0:T(8,128)(2,1)S(1)}, bf16[64,1024]{1,0:T(8,128)(2,1)S(1)}, u32[]{:S(2)}, u32[]{:S(2)}) %collective-permute-start.12) | collective-permute-done | bytes 131104 | tf_op jit(solution)/shard_map/ppermute | solution.py:20
  18.3 2.6 %up_gate.6 = (bf16[2,32,3584]{2,1,0:T(8,128)(2,1)S(1)}, f32[2,32,3584]{2,1,0:T(8,128)S(1)}) custom-call(s32[1]{0:T(128)} %bitcast.me_ref, bf16[64,1024]{1,0:T(8,128)(2,1)S(1)} %collective-permute-done.12.refs_0_, bf16[1024,3584]{1,0:T(8,128)(2,1)S(1)} %copy-done, bf16[1024,3584]{1,0:T(8,128)(2,1)S(1)} %copy-done.1), custom_call_target="tpu_custom_call" | custom-call | flops 939524096 | bytes 14680064 | tf_op jit(solution)/shard_map/up_gate/pallas_call | solution.py:75
  21.0 4.6 %collective-permute-done.19.refs_0_ = bf16[64,1024]{1,0:T(8,128)(2,1)S(1)} collective-permute-done((bf16[64,1024]{1,0:T(8,128)(2,1)S(1)}, bf16[64,1024]{1,0:T(8,128)(2,1)S(1)}, u32[]{:S(2)}, u32[]{:S(2)}) %collective-permute-start.19) | collective-permute-done | bytes 131104 | tf_op jit(solution)/shard_map/ppermute | solution.py:20
  25.5 2.6 %up_gate.7 = (bf16[2,32,3584]{2,1,0:T(8,128)(2,1)S(1)}, f32[2,32,3584]{2,1,0:T(8,128)S(1)}) custom-call(s32[1]{0:T(128)} %bitcast.me_ref, bf16[64,1024]{1,0:T(8,128)(2,1)S(1)} %collective-permute-done.19.refs_0_, bf16[1024,3584]{1,0:T(8,128)(2,1)S(1)} %copy-done, bf16[1024,3584]{1,0:T(8,128)(2,1)S(1)} %copy-done.1), custom_call_target="tpu_custom_call" | custom-call | flops 939524096 | bytes 14680064 | tf_op jit(solution)/shard_map/up_gate/pallas_call | solution.py:75
  28.2 2.6 %up_gate.5 = (bf16[2,32,3584]{2,1,0:T(8,128)(2,1)S(1)}, f32[2,32,3584]{2,1,0:T(8,128)S(1)}) custom-call(s32[1]{0:T(128)} %bitcast.me_ref, bf16[64,1024]{1,0:T(8,128)(2,1)S(1)} %collective-permute-done.5.refs_0_, bf16[1024,3584]{1,0:T(8,128)(2,1)S(1)} %copy-done, bf16[1024,3584]{1,0:T(8,128)(2,1)S(1)} %copy-done.1), custom_call_target="tpu_custom_call" | custom-call | flops 939524096 | bytes 14680064 | tf_op jit(solution)/shard_map/up_gate/pallas_call | solution.py:75
  31.4 1.6 %collective-permute-start.1 = (bf16[2,16,3584]{2,1,0:T(8,128)(2,1)S(1)}, bf16[2,16,3584]{2,1,0:T(8,128)(2,1)S(1)}, u32[]{:S(2)}, u32[]{:S(2)}) collective-permute-start(bf16[2,16,3584]{2,1,0:T(8,128)(2,1)S(1)} %add_convert_fusion.3), channel_id=1, source_target_pairs={{0,2},{1,3},{2,0},{3,1},{4,6},{5,7},{6,4},{7,5},{8,10},{9,11},{10,... | collective-permute-start | bytes 688136 | tf_op jit(solution)/shard_map/ppermute | solution.py:20
  33.0 0.6 collective-permute-start.14
  33.7 1.6 %collective-permute-start.21 = (bf16[2,16,3584]{2,1,0:T(8,128)(2,1)S(1)}, bf16[2,16,3584]{2,1,0:T(8,128)(2,1)S(1)}, u32[]{:S(2)}, u32[]{:S(2)}) collective-permute-start(bf16[2,16,3584]{2,1,0:T(8,128)(2,1)S(1)} %add_convert_fusion), channel_id=1, source_target_pairs={{0,2},{1,3},{2,0},{3,1},{4,6},{5,7},{6,4},{7,5},{8,10},{9,11},{10,... | collective-permute-start | bytes 688136 | tf_op jit(solution)/shard_map/ppermute | solution.py:20
  35.9 4.1 %collective-permute-done.1 = bf16[2,16,3584]{2,1,0:T(8,128)(2,1)S(1)} collective-permute-done((bf16[2,16,3584]{2,1,0:T(8,128)(2,1)S(1)}, bf16[2,16,3584]{2,1,0:T(8,128)(2,1)S(1)}, u32[]{:S(2)}, u32[]{:S(2)}) %collective-permute-start.1) | collective-permute-done | bytes 229408 | tf_op jit(solution)/shard_map/ppermute | solution.py:20
  40.0 4.8 %collective-permute-done.14 = bf16[2,16,3584]{2,1,0:T(8,128)(2,1)S(1)} collective-permute-done((bf16[2,16,3584]{2,1,0:T(8,128)(2,1)S(1)}, bf16[2,16,3584]{2,1,0:T(8,128)(2,1)S(1)}, u32[]{:S(2)}, u32[]{:S(2)}) %collective-permute-start.14) | collective-permute-done | bytes 229408 | tf_op jit(solution)/shard_map/ppermute | solution.py:20
  45.1 1.6 %collective-permute-start.15 = (bf16[16,3584]{1,0:T(8,128)(2,1)S(1)}, bf16[16,3584]{1,0:T(8,128)(2,1)S(1)}, u32[]{:S(2)}, u32[]{:S(2)}) collective-permute-start(bf16[16,3584]{1,0:T(8,128)(2,1)S(1)} %fusion.3.h0), channel_id=1, source_target_pairs={{0,2},{1,3},{2,0},{3,1},{4,6},{5,7},{6,4},{7,5},{8,10},{9,11},{10,... | collective-permute-start | bytes 344072 | tf_op jit(solution)/shard_map/ppermute | solution.py:20
  46.7 3.1 %collective-permute-done.21 = bf16[2,16,3584]{2,1,0:T(8,128)(2,1)S(1)} collective-permute-done((bf16[2,16,3584]{2,1,0:T(8,128)(2,1)S(1)}, bf16[2,16,3584]{2,1,0:T(8,128)(2,1)S(1)}, u32[]{:S(2)}, u32[]{:S(2)}) %collective-permute-start.21) | collective-permute-done | bytes 229408 | tf_op jit(solution)/shard_map/ppermute | solution.py:20
  49.9 1.6 %collective-permute-start.22 = (bf16[16,3584]{1,0:T(8,128)(2,1)S(1)}, bf16[16,3584]{1,0:T(8,128)(2,1)S(1)}, u32[]{:S(2)}, u32[]{:S(2)}) collective-permute-start(bf16[16,3584]{1,0:T(8,128)(2,1)S(1)} %fusion.1.h0), channel_id=1, source_target_pairs={{0,2},{1,3},{2,0},{3,1},{4,6},{5,7},{6,4},{7,5},{8,10},{9,11},{10,... | collective-permute-start | bytes 344072 | tf_op jit(solution)/shard_map/ppermute | solution.py:20
  51.5 3.2 %collective-permute-done.7 = bf16[2,16,3584]{2,1,0:T(8,128)(2,1)S(1)} collective-permute-done((bf16[2,16,3584]{2,1,0:T(8,128)(2,1)S(1)}, bf16[2,16,3584]{2,1,0:T(8,128)(2,1)S(1)}, u32[]{:S(2)}, u32[]{:S(2)}) %collective-permute-start.7) | collective-permute-done | bytes 229408 | tf_op jit(solution)/shard_map/ppermute | solution.py:20
  54.8 1.6 %collective-permute-start.8 = (bf16[16,3584]{1,0:T(8,128)(2,1)S(1)}, bf16[16,3584]{1,0:T(8,128)(2,1)S(1)}, u32[]{:S(2)}, u32[]{:S(2)}) collective-permute-start(bf16[16,3584]{1,0:T(8,128)(2,1)S(1)} %fusion.5.h0), channel_id=1, source_target_pairs={{0,2},{1,3},{2,0},{3,1},{4,6},{5,7},{6,4},{7,5},{8,10},{9,11},{10,... | collective-permute-start | bytes 344072 | tf_op jit(solution)/shard_map/ppermute | solution.py:20
  56.4 0.8 collective-permute-done.15.h2
  57.2 1.6 %collective-permute-start.2 = (bf16[16,3584]{1,0:T(8,128)(2,1)S(1)}, bf16[16,3584]{1,0:T(8,128)(2,1)S(1)}, u32[]{:S(2)}, u32[]{:S(2)}) collective-permute-start(bf16[16,3584]{1,0:T(8,128)(2,1)S(1)} %fusion.7.h0), channel_id=1, source_target_pairs={{0,2},{1,3},{2,0},{3,1},{4,6},{5,7},{6,4},{7,5},{8,10},{9,11},{10,... | collective-permute-start | bytes 344072 | tf_op jit(solution)/shard_map/ppermute | solution.py:20
  59.6 2.2 %collective-permute-done.8.h2 = bf16[16,3584]{1,0:T(8,128)(2,1)S(1)} collective-permute-done((bf16[16,3584]{1,0:T(8,128)(2,1)S(1)}, bf16[16,3584]{1,0:T(8,128)(2,1)S(1)}, u32[]{:S(2)}, u32[]{:S(2)}) %collective-permute-start.8) | collective-permute-done | bytes 114720 | tf_op jit(solution)/shard_map/ppermute | solution.py:20
  62.4 1.4 %down.6 = bf16[64,1024]{1,0:T(8,128)(2,1)S(1)} custom-call(s32[1]{0:T(128)} %bitcast.me_ref, bf16[16,3584]{1,0:T(8,128)(2,1)S(1)} %fusion.3.h0, bf16[16,3584]{1,0:T(8,128)(2,1)S(1)} %collective-permute-done.15.h2, bf16[16,3584]{1,0:T(8,128)(2,1)S(1)} %collective-permute-done.16.h1, bf16[16,3584]{1,0:T(8,128)(2,1)S(1)} %collective-permute-done.17.h3, ...), custom_call_target="tpu_custom_call" | custom-call | flops 469762048 | bytes 7340032 | tf_op jit(solution)/shard_map/down/pallas_call | solution.py:111
  64.4 2.5 %collective-permute-start.18 = (bf16[64,1024]{1,0:T(8,128)(2,1)S(1)}, bf16[64,1024]{1,0:T(8,128)(2,1)S(1)}, u32[]{:S(2)}, u32[]{:S(2)}) collective-permute-start(bf16[64,1024]{1,0:T(8,128)(2,1)S(1)} %down.6), channel_id=1, source_target_pairs={{0,12},{4,8},{8,4},{12,0},{1,13},{5,9},{9,5},{13,1},{2,14},{6,10},... | collective-permute-start | bytes 393224 | tf_op jit(solution)/shard_map/ppermute | solution.py:20
  66.8 1.4 %down.7 = bf16[64,1024]{1,0:T(8,128)(2,1)S(1)} custom-call(s32[1]{0:T(128)} %bitcast.me_ref, bf16[16,3584]{1,0:T(8,128)(2,1)S(1)} %fusion.1.h0, bf16[16,3584]{1,0:T(8,128)(2,1)S(1)} %collective-permute-done.22.h2, bf16[16,3584]{1,0:T(8,128)(2,1)S(1)} %collective-permute-done.23.h1, bf16[16,3584]{1,0:T(8,128)(2,1)S(1)} %collective-permute-done.24.h3, ...), custom_call_target="tpu_custom_call" | custom-call | flops 469762048 | bytes 7340032 | tf_op jit(solution)/shard_map/down/pallas_call | solution.py:111
  68.5 1.4 %down.5 = bf16[64,1024]{1,0:T(8,128)(2,1)S(1)} custom-call(s32[1]{0:T(128)} %bitcast.me_ref, bf16[16,3584]{1,0:T(8,128)(2,1)S(1)} %fusion.5.h0, bf16[16,3584]{1,0:T(8,128)(2,1)S(1)} %collective-permute-done.8.h2, bf16[16,3584]{1,0:T(8,128)(2,1)S(1)} %collective-permute-done.9.h1, bf16[16,3584]{1,0:T(8,128)(2,1)S(1)} %collective-permute-done.10.h3, ...), custom_call_target="tpu_custom_call" | custom-call | flops 469762048 | bytes 7340032 | tf_op jit(solution)/shard_map/down/pallas_call | solution.py:111
  69.8 1.8 %collective-permute-start.11 = (bf16[64,1024]{1,0:T(8,128)(2,1)S(1)}, bf16[64,1024]{1,0:T(8,128)(2,1)S(1)}, u32[]{:S(2)}, u32[]{:S(2)}) collective-permute-start(bf16[64,1024]{1,0:T(8,128)(2,1)S(1)} %down.5), channel_id=1, source_target_pairs={{0,4},{4,0},{8,12},{12,8},{1,5},{5,1},{9,13},{13,9},{2,6},{6,2},{1... | collective-permute-start | bytes 393224 | tf_op jit(solution)/shard_map/ppermute | solution.py:20
  71.7 1.4 %down.4 = f32[64,1024]{1,0:T(8,128)S(1)} custom-call(s32[1]{0:T(128)} %bitcast.me_ref, bf16[16,3584]{1,0:T(8,128)(2,1)S(1)} %fusion.7.h0, bf16[16,3584]{1,0:T(8,128)(2,1)S(1)} %collective-permute-done.2.h2, bf16[16,3584]{1,0:T(8,128)(2,1)S(1)} %collective-permute-done.3.h1, bf16[16,3584]{1,0:T(8,128)(2,1)S(1)} %collective-permute-done.4.h3, ...), custom_call_target="tpu_custom_call" | custom-call | flops 469762048 | bytes 7340032 | tf_op jit(solution)/shard_map/down/pallas_call | solution.py:111
  73.1 5.8 %collective-permute-done.25 = bf16[64,1024]{1,0:T(8,128)(2,1)S(1)} collective-permute-done((bf16[64,1024]{1,0:T(8,128)(2,1)S(1)}, bf16[64,1024]{1,0:T(8,128)(2,1)S(1)}, u32[]{:S(2)}, u32[]{:S(2)}) %collective-permute-start.25) | collective-permute-done | bytes 131104 | tf_op jit(solution)/shard_map/ppermute | solution.py:20
  78.9 0.7 add_convert_fusion.4
  (53 shorter events, 4.8 us)
Async XLA Ops:
  0.0 0.9 %copy-start.2 = (bf16[64,1024]{1,0:T(8,128)(2,1)S(1)}, bf16[64,1024]{1,0:T(8,128)(2,1)}, u32[]{:S(2)}) copy-start(bf16[64,1024]{1,0:T(8,128)(2,1)} %refs_0_.1) | copy-start | bytes 393220
  0.9 3.1 %copy-start = (bf16[1024,3584]{1,0:T(8,128)(2,1)S(1)}, bf16[1024,3584]{1,0:T(8,128)(2,1)}, u32[]{:S(2)}) copy-start(bf16[1024,3584]{1,0:T(8,128)(2,1)} %refs_1_.7) | copy-start | bytes 22020100
  0.9 5.2 %copy-start.1 = (bf16[1024,3584]{1,0:T(8,128)(2,1)S(1)}, bf16[1024,3584]{1,0:T(8,128)(2,1)}, u32[]{:S(2)}) copy-start(bf16[1024,3584]{1,0:T(8,128)(2,1)} %refs_2_.7) | copy-start | bytes 22020100
  8.7 22.7 %collective-permute-start = (bf16[2,32,3584]{2,1,0:T(8,128)(2,1)S(1)}, bf16[2,32,3584]{2,1,0:T(8,128)(2,1)S(1)}, u32[]{:S(2)}, u32[]{:S(2)}) collective-permute-start(bf16[2,32,3584]{2,1,0:T(8,128)(2,1)S(1)} %get-tuple-element.14), channel_id=1, source_target_pairs={{0,1},{1,0},{2,3},{3,2},{4,5},{5,4},{6,7},{7,6},{8,9},{9,8},{10,11... | collective-permute-start | bytes 1376264 | tf_op jit(solution)/shard_map/ppermute | solution.py:20
  9.2 9.1 %collective-permute-start.12 = (bf16[64,1024]{1,0:T(8,128)(2,1)S(1)}, bf16[64,1024]{1,0:T(8,128)(2,1)S(1)}, u32[]{:S(2)}, u32[]{:S(2)}) collective-permute-start(bf16[64,1024]{1,0:T(8,128)(2,1)S(1)} %copy-done.2), channel_id=1, source_target_pairs={{0,12},{4,8},{8,4},{12,0},{1,13},{5,9},{9,5},{13,1},{2,14},{6,10},... | collective-permute-start | bytes 393224 | tf_op jit(solution)/shard_map/ppermute | solution.py:20
  13.9 11.7 %collective-permute-start.19 = (bf16[64,1024]{1,0:T(8,128)(2,1)S(1)}, bf16[64,1024]{1,0:T(8,128)(2,1)S(1)}, u32[]{:S(2)}, u32[]{:S(2)}) collective-permute-start(bf16[64,1024]{1,0:T(8,128)(2,1)S(1)} %copy-done.2), channel_id=1, source_target_pairs={{0,8},{4,12},{8,0},{12,4},{1,9},{5,13},{9,1},{13,5},{2,10},{6,14},... | collective-permute-start | bytes 393224 | tf_op jit(solution)/shard_map/ppermute | solution.py:20
  13.9 14.3 %collective-permute-start.5 = (bf16[64,1024]{1,0:T(8,128)(2,1)S(1)}, bf16[64,1024]{1,0:T(8,128)(2,1)S(1)}, u32[]{:S(2)}, u32[]{:S(2)}) collective-permute-start(bf16[64,1024]{1,0:T(8,128)(2,1)S(1)} %copy-done.2), channel_id=1, source_target_pairs={{0,4},{4,0},{8,12},{12,8},{1,5},{5,1},{9,13},{13,9},{2,6},{6,2},{1... | collective-permute-start | bytes 393224 | tf_op jit(solution)/shard_map/ppermute | solution.py:20
  20.9 12.1 %collective-permute-start.13 = (bf16[2,32,3584]{2,1,0:T(8,128)(2,1)S(1)}, bf16[2,32,3584]{2,1,0:T(8,128)(2,1)S(1)}, u32[]{:S(2)}, u32[]{:S(2)}) collective-permute-start(bf16[2,32,3584]{2,1,0:T(8,128)(2,1)S(1)} %get-tuple-element.18), channel_id=1, source_target_pairs={{0,1},{1,0},{2,3},{3,2},{4,5},{5,4},{6,7},{7,6},{8,9},{9,8},{10,11... | collective-permute-start | bytes 1376264 | tf_op jit(solution)/shard_map/ppermute | solution.py:20
  28.1 34.3 %slice-start = ((s8[7340032]{0:T(1024)(128)(4,1)}), s8[4194304]{0:T(1024)(128)(4,1)S(1)}, s32[]{:S(2)}) async-start(s8[7340032]{0:T(1024)(128)(4,1)} %bitcast.41), calls=%async_computation | async-start | bytes 8388608
  28.1 34.2 %slice-start.1 = ((s8[7340032]{0:T(1024)(128)(4,1)}), s8[3145728]{0:T(1024)(128)(4,1)S(1)}, s32[]{:S(2)}) async-start(s8[7340032]{0:T(1024)(128)(4,1)} %bitcast.41), calls=%async_computation.1 | async-start | bytes 6291456
  28.1 5.5 %collective-permute-start.20 = (bf16[2,32,3584]{2,1,0:T(8,128)(2,1)S(1)}, bf16[2,32,3584]{2,1,0:T(8,128)(2,1)S(1)}, u32[]{:S(2)}, u32[]{:S(2)}) collective-permute-start(bf16[2,32,3584]{2,1,0:T(8,128)(2,1)S(1)} %get-tuple-element.20), channel_id=1, source_target_pairs={{0,1},{1,0},{2,3},{3,2},{4,5},{5,4},{6,7},{7,6},{8,9},{9,8},{10,11... | collective-permute-start | bytes 1376264 | tf_op jit(solution)/shard_map/ppermute | solution.py:20
  30.8 4.4 %collective-permute-start.6 = (bf16[2,32,3584]{2,1,0:T(8,128)(2,1)S(1)}, bf16[2,32,3584]{2,1,0:T(8,128)(2,1)S(1)}, u32[]{:S(2)}, u32[]{:S(2)}) collective-permute-start(bf16[2,32,3584]{2,1,0:T(8,128)(2,1)S(1)} %get-tuple-element.16), channel_id=1, source_target_pairs={{0,1},{1,0},{2,3},{3,2},{4,5},{5,4},{6,7},{7,6},{8,9},{9,8},{10,11... | collective-permute-start | bytes 1376264 | tf_op jit(solution)/shard_map/ppermute | solution.py:20
  31.4 8.5 %collective-permute-start.1 = (bf16[2,16,3584]{2,1,0:T(8,128)(2,1)S(1)}, bf16[2,16,3584]{2,1,0:T(8,128)(2,1)S(1)}, u32[]{:S(2)}, u32[]{:S(2)}) collective-permute-start(bf16[2,16,3584]{2,1,0:T(8,128)(2,1)S(1)} %add_convert_fusion.3), channel_id=1, source_target_pairs={{0,2},{1,3},{2,0},{3,1},{4,6},{5,7},{6,4},{7,5},{8,10},{9,11},{10,... | collective-permute-start | bytes 688136 | tf_op jit(solution)/shard_map/ppermute | solution.py:20
  33.0 11.9 %collective-permute-start.14 = (bf16[2,16,3584]{2,1,0:T(8,128)(2,1)S(1)}, bf16[2,16,3584]{2,1,0:T(8,128)(2,1)S(1)}, u32[]{:S(2)}, u32[]{:S(2)}) collective-permute-start(bf16[2,16,3584]{2,1,0:T(8,128)(2,1)S(1)} %add_convert_fusion.1), channel_id=1, source_target_pairs={{0,2},{1,3},{2,0},{3,1},{4,6},{5,7},{6,4},{7,5},{8,10},{9,11},{10,... | collective-permute-start | bytes 688136 | tf_op jit(solution)/shard_map/ppermute | solution.py:20
  33.7 16.1 %collective-permute-start.21 = (bf16[2,16,3584]{2,1,0:T(8,128)(2,1)S(1)}, bf16[2,16,3584]{2,1,0:T(8,128)(2,1)S(1)}, u32[]{:S(2)}, u32[]{:S(2)}) collective-permute-start(bf16[2,16,3584]{2,1,0:T(8,128)(2,1)S(1)} %add_convert_fusion), channel_id=1, source_target_pairs={{0,2},{1,3},{2,0},{3,1},{4,6},{5,7},{6,4},{7,5},{8,10},{9,11},{10,... | collective-permute-start | bytes 688136 | tf_op jit(solution)/shard_map/ppermute | solution.py:20
  35.3 19.4 %collective-permute-start.7 = (bf16[2,16,3584]{2,1,0:T(8,128)(2,1)S(1)}, bf16[2,16,3584]{2,1,0:T(8,128)(2,1)S(1)}, u32[]{:S(2)}, u32[]{:S(2)}) collective-permute-start(bf16[2,16,3584]{2,1,0:T(8,128)(2,1)S(1)} %add_convert_fusion.2), channel_id=1, source_target_pairs={{0,2},{1,3},{2,0},{3,1},{4,6},{5,7},{6,4},{7,5},{8,10},{9,11},{10,... | collective-permute-start | bytes 688136 | tf_op jit(solution)/shard_map/ppermute | solution.py:20
  45.0 13.8 %collective-permute-start.16 = (bf16[16,3584]{1,0:T(8,128)(2,1)S(1)}, bf16[16,3584]{1,0:T(8,128)(2,1)S(1)}, u32[]{:S(2)}, u32[]{:S(2)}) collective-permute-start(bf16[16,3584]{1,0:T(8,128)(2,1)S(1)} %fusion.3.h0), channel_id=1, source_target_pairs={{0,1},{1,0},{2,3},{3,2},{4,5},{5,4},{6,7},{7,6},{8,9},{9,8},{10,11... | collective-permute-start | bytes 344072 | tf_op jit(solution)/shard_map/ppermute | solution.py:20
  45.1 12.1 %collective-permute-start.15 = (bf16[16,3584]{1,0:T(8,128)(2,1)S(1)}, bf16[16,3584]{1,0:T(8,128)(2,1)S(1)}, u32[]{:S(2)}, u32[]{:S(2)}) collective-permute-start(bf16[16,3584]{1,0:T(8,128)(2,1)S(1)} %fusion.3.h0), channel_id=1, source_target_pairs={{0,2},{1,3},{2,0},{3,1},{4,6},{5,7},{6,4},{7,5},{8,10},{9,11},{10,... | collective-permute-start | bytes 344072 | tf_op jit(solution)/shard_map/ppermute | solution.py:20
  49.9 9.7 %collective-permute-start.22 = (bf16[16,3584]{1,0:T(8,128)(2,1)S(1)}, bf16[16,3584]{1,0:T(8,128)(2,1)S(1)}, u32[]{:S(2)}, u32[]{:S(2)}) collective-permute-start(bf16[16,3584]{1,0:T(8,128)(2,1)S(1)} %fusion.1.h0), channel_id=1, source_target_pairs={{0,2},{1,3},{2,0},{3,1},{4,6},{5,7},{6,4},{7,5},{8,10},{9,11},{10,... | collective-permute-start | bytes 344072 | tf_op jit(solution)/shard_map/ppermute | solution.py:20
  54.8 7.0 %collective-permute-start.8 = (bf16[16,3584]{1,0:T(8,128)(2,1)S(1)}, bf16[16,3584]{1,0:T(8,128)(2,1)S(1)}, u32[]{:S(2)}, u32[]{:S(2)}) collective-permute-start(bf16[16,3584]{1,0:T(8,128)(2,1)S(1)} %fusion.5.h0), channel_id=1, source_target_pairs={{0,2},{1,3},{2,0},{3,1},{4,6},{5,7},{6,4},{7,5},{8,10},{9,11},{10,... | collective-permute-start | bytes 344072 | tf_op jit(solution)/shard_map/ppermute | solution.py:20
  57.2 4.7 %collective-permute-start.17 = (bf16[16,3584]{1,0:T(8,128)(2,1)S(1)}, bf16[16,3584]{1,0:T(8,128)(2,1)S(1)}, u32[]{:S(2)}, u32[]{:S(2)}) collective-permute-start(bf16[16,3584]{1,0:T(8,128)(2,1)S(1)} %collective-permute-done.15.h2), channel_id=1, source_target_pairs={{0,1},{1,0},{2,3},{3,2},{4,5},{5,4},{6,7},{7,6},{8,9},{9,8},{10,11... | collective-permute-start | bytes 344072 | tf_op jit(solution)/shard_map/ppermute | solution.py:20
  57.2 6.5 %collective-permute-start.2 = (bf16[16,3584]{1,0:T(8,128)(2,1)S(1)}, bf16[16,3584]{1,0:T(8,128)(2,1)S(1)}, u32[]{:S(2)}, u32[]{:S(2)}) collective-permute-start(bf16[16,3584]{1,0:T(8,128)(2,1)S(1)} %fusion.7.h0), channel_id=1, source_target_pairs={{0,2},{1,3},{2,0},{3,1},{4,6},{5,7},{6,4},{7,5},{8,10},{9,11},{10,... | collective-permute-start | bytes 344072 | tf_op jit(solution)/shard_map/ppermute | solution.py:20
  58.8 5.1 %collective-permute-start.23 = (bf16[16,3584]{1,0:T(8,128)(2,1)S(1)}, bf16[16,3584]{1,0:T(8,128)(2,1)S(1)}, u32[]{:S(2)}, u32[]{:S(2)}) collective-permute-start(bf16[16,3584]{1,0:T(8,128)(2,1)S(1)} %fusion.1.h0), channel_id=1, source_target_pairs={{0,1},{1,0},{2,3},{3,2},{4,5},{5,4},{6,7},{7,6},{8,9},{9,8},{10,11... | collective-permute-start | bytes 344072 | tf_op jit(solution)/shard_map/ppermute | solution.py:20
  59.6 4.7 %collective-permute-start.24 = (bf16[16,3584]{1,0:T(8,128)(2,1)S(1)}, bf16[16,3584]{1,0:T(8,128)(2,1)S(1)}, u32[]{:S(2)}, u32[]{:S(2)}) collective-permute-start(bf16[16,3584]{1,0:T(8,128)(2,1)S(1)} %collective-permute-done.22.h2), channel_id=1, source_target_pairs={{0,1},{1,0},{2,3},{3,2},{4,5},{5,4},{6,7},{7,6},{8,9},{9,8},{10,11... | collective-permute-start | bytes 344072 | tf_op jit(solution)/shard_map/ppermute | solution.py:20
  61.9 6.4 %collective-permute-start.9 = (bf16[16,3584]{1,0:T(8,128)(2,1)S(1)}, bf16[16,3584]{1,0:T(8,128)(2,1)S(1)}, u32[]{:S(2)}, u32[]{:S(2)}) collective-permute-start(bf16[16,3584]{1,0:T(8,128)(2,1)S(1)} %fusion.5.h0), channel_id=1, source_target_pairs={{0,1},{1,0},{2,3},{3,2},{4,5},{5,4},{6,7},{7,6},{8,9},{9,8},{10,11... | collective-permute-start | bytes 344072 | tf_op jit(solution)/shard_map/ppermute | solution.py:20
  61.9 6.6 %collective-permute-start.10 = (bf16[16,3584]{1,0:T(8,128)(2,1)S(1)}, bf16[16,3584]{1,0:T(8,128)(2,1)S(1)}, u32[]{:S(2)}, u32[]{:S(2)}) collective-permute-start(bf16[16,3584]{1,0:T(8,128)(2,1)S(1)} %collective-permute-done.8.h2), channel_id=1, source_target_pairs={{0,1},{1,0},{2,3},{3,2},{4,5},{5,4},{6,7},{7,6},{8,9},{9,8},{10,11... | collective-permute-start | bytes 344072 | tf_op jit(solution)/shard_map/ppermute | solution.py:20
  63.8 7.9 %collective-permute-start.3 = (bf16[16,3584]{1,0:T(8,128)(2,1)S(1)}, bf16[16,3584]{1,0:T(8,128)(2,1)S(1)}, u32[]{:S(2)}, u32[]{:S(2)}) collective-permute-start(bf16[16,3584]{1,0:T(8,128)(2,1)S(1)} %fusion.7.h0), channel_id=1, source_target_pairs={{0,1},{1,0},{2,3},{3,2},{4,5},{5,4},{6,7},{7,6},{8,9},{9,8},{10,11... | collective-permute-start | bytes 344072 | tf_op jit(solution)/shard_map/ppermute | solution.py:20
  63.9 7.8 %collective-permute-start.4 = (bf16[16,3584]{1,0:T(8,128)(2,1)S(1)}, bf16[16,3584]{1,0:T(8,128)(2,1)S(1)}, u32[]{:S(2)}, u32[]{:S(2)}) collective-permute-start(bf16[16,3584]{1,0:T(8,128)(2,1)S(1)} %collective-permute-done.2.h2), channel_id=1, source_target_pairs={{0,1},{1,0},{2,3},{3,2},{4,5},{5,4},{6,7},{7,6},{8,9},{9,8},{10,11... | collective-permute-start | bytes 344072 | tf_op jit(solution)/shard_map/ppermute | solution.py:20
  64.4 8.7 %collective-permute-start.18 = (bf16[64,1024]{1,0:T(8,128)(2,1)S(1)}, bf16[64,1024]{1,0:T(8,128)(2,1)S(1)}, u32[]{:S(2)}, u32[]{:S(2)}) collective-permute-start(bf16[64,1024]{1,0:T(8,128)(2,1)S(1)} %down.6), channel_id=1, source_target_pairs={{0,12},{4,8},{8,4},{12,0},{1,13},{5,9},{9,5},{13,1},{2,14},{6,10},... | collective-permute-start | bytes 393224 | tf_op jit(solution)/shard_map/ppermute | solution.py:20
  68.2 10.7 %collective-permute-start.25 = (bf16[64,1024]{1,0:T(8,128)(2,1)S(1)}, bf16[64,1024]{1,0:T(8,128)(2,1)S(1)}, u32[]{:S(2)}, u32[]{:S(2)}) collective-permute-start(bf16[64,1024]{1,0:T(8,128)(2,1)S(1)} %down.7), channel_id=1, source_target_pairs={{0,8},{4,12},{8,0},{12,4},{1,9},{5,13},{9,1},{13,5},{2,10},{6,14},... | collective-permute-start | bytes 393224 | tf_op jit(solution)/shard_map/ppermute | solution.py:20
  69.8 9.0 %collective-permute-start.11 = (bf16[64,1024]{1,0:T(8,128)(2,1)S(1)}, bf16[64,1024]{1,0:T(8,128)(2,1)S(1)}, u32[]{:S(2)}, u32[]{:S(2)}) collective-permute-start(bf16[64,1024]{1,0:T(8,128)(2,1)S(1)} %down.5), channel_id=1, source_target_pairs={{0,4},{4,0},{8,12},{12,8},{1,5},{5,1},{9,13},{13,9},{2,6},{6,2},{1... | collective-permute-start | bytes 393224 | tf_op jit(solution)/shard_map/ppermute | solution.py:20

commit v2 on v1

--- a/solution.py
+++ b/solution.py
@@ -9,6 +9,8 @@
 
 
 CHUNKS = ((0,), (1,), (3,), (2,))
+FAR = 2
+SPLIT = {0: 2}
 ORDER = (3, 1, 2, 0)
 MIB = 1024 * 1024
 VMEM = pl.BlockSpec(memory_space=pltpu.VMEM)
@@ -50,30 +52,31 @@
         compiler_params=pltpu.CompilerParams(vmem_limit_bytes=12 * MIB),
         cost_estimate=pl.CostEstimate(flops=10**10, bytes_accessed=0, transcendentals=0),
         name="sort",
-    )(me, *xs)
+    )(me, *[pltpu.with_memory_space_constraint(x, pltpu.HBM) for x in xs])
 
 
-def up_gate_kernel(me_ref, *refs, blocks):
+def up_gate_kernel(me_ref, *refs, blocks, first):
     x_refs, (g_ref, u_ref, send_ref, keep_ref, *scratch) = refs[:blocks], refs[blocks:]
     if scratch:
         sort_rows(me_ref[0], x_refs, scratch[0])
     x = (scratch or x_refs)[0][...]
     half = x.shape[0] // 2
-    hidden = g_ref.shape[1]
-    width = width_of(hidden)
-    for j in range(hidden // width):
+    share = send_ref.shape[2]
+    width = width_of(share)
+    for j in range(share // width):
         cols = slice(j * width, (j + 1) * width)
+        taken = slice(first + j * width, first + (j + 1) * width)
         for i, w_ref in enumerate((g_ref, u_ref)):
-            y = jnp.dot(x, w_ref[:, cols], preferred_element_type=jnp.float32)
+            y = jnp.dot(x, w_ref[:, taken], preferred_element_type=jnp.float32)
             send_ref[i, :, cols] = y[:half].astype(send_ref.dtype)
             keep_ref[i, :, cols] = y[half:]
 
 
-def up_gate(me, xs, gate, up, ordered):
-    depth, hidden = gate.shape
+def up_gate(me, xs, gate, up, ordered, piece, pieces):
+    depth, hidden = gate.shape[0], gate.shape[1] // pieces
     rows = xs[0].shape[0] * len(xs)
     return pl.pallas_call(
-        functools.partial(up_gate_kernel, blocks=len(xs)),
+        functools.partial(up_gate_kernel, blocks=len(xs), first=piece * hidden),
         in_specs=[SMEM] + [VMEM] * (len(xs) + 2),
         out_specs=[VMEM] * 2,
         out_shape=[
@@ -89,7 +92,8 @@
     )(me, *xs, held(gate), held(up))
 
 
-def down_kernel(me_ref, h0, h2, h1, h3, w_ref, *outs):
+def down_kernel(me_ref, h0, h2, h1, h3, w_ref, *refs, blocks):
+    outs, adds = refs[-blocks:], refs[:-blocks]
     me = me_ref[0]
     h = jnp.concatenate([h0[...], h2[...], h1[...], h3[...]], axis=0)
     part = outs[0].shape[0] // len(ORDER)
@@ -102,15 +106,18 @@
             at = pl.multiple_of((me ^ r) * part, part)
             for b, out in enumerate(outs):
                 first = (i * len(outs) + b) * part
-                out[pl.ds(at, part), cols] = y[first : first + part].astype(out.dtype)
+                value = y[first : first + part]
+                if adds:
+                    value += adds[b][pl.ds(at, part), cols].astype(jnp.float32)
+                out[pl.ds(at, part), cols] = value.astype(out.dtype)
 
 
-def down(me, hs, weight, block_rows, kinds):
+def down(me, hs, weight, block_rows, kinds, adds):
     hidden, depth = weight.shape
     rows = block_rows * len(kinds)
     return pl.pallas_call(
-        down_kernel,
-        in_specs=[SMEM] + [VMEM] * 5,
+        functools.partial(down_kernel, blocks=len(kinds)),
+        in_specs=[SMEM] + [VMEM] * (5 + len(adds)),
         out_specs=[VMEM] * len(kinds),
         out_shape=[jax.ShapeDtypeStruct((block_rows, depth), kind) for kind in kinds],
         compiler_params=pltpu.CompilerParams(vmem_limit_bytes=12 * MIB),
@@ -118,7 +125,7 @@
             flops=2 * rows * depth * hidden, bytes_accessed=2 * depth * hidden, transcendentals=0
         ),
         name="down",
-    )(me, *hs, held(weight))
+    )(me, *hs, held(weight), *adds)
 
 
 def steps(tokens, gate_weight, up_weight, down_weight):
@@ -133,28 +140,39 @@
             if s:
                 blocks[s] = flip(tokens, "grid", s)
     total = None
-    arrived = []
+    arrived, relayed = [], {}
     for number, chunk in enumerate(chunks):
         xs = [blocks[s] for s in chunk]
         if number == 0:
             xs = [sort(me, xs)]
-        send, keep = up_gate(me, xs, gate_weight, up_weight, number == 0)
-        part = keep.shape[1] // 2
-        recv = flip(send, "depth", 1)
-        across = (keep[:, :part] + recv[:, :part].astype(jnp.float32)).astype(jnp.bfloat16)
-        crossed = flip(across, "depth", 2)
-        both = keep[:, part:] + recv[:, part:].astype(jnp.float32) + crossed.astype(jnp.float32)
-        mine = (jax.nn.silu(both[0]) * both[1]).astype(jnp.bfloat16)
+        pieces = SPLIT.get(number, 1) if gate_weight.shape[1] % 256 == 0 else 1
+        sums = []
+        for piece in range(pieces):
+            send, keep = up_gate(me, xs, gate_weight, up_weight, number == 0, piece, pieces)
+            part = keep.shape[1] // 2
+            recv = flip(send, "depth", 1)
+            across = (keep[:, :part] + recv[:, :part].astype(jnp.float32)).astype(jnp.bfloat16)
+            crossed = flip(across, "depth", 2)
+            sums.append((keep, recv, crossed))
+        mine = []
+        for keep, recv, crossed in sums:
+            both = keep[:, part:] + recv[:, part:].astype(jnp.float32) + crossed.astype(jnp.float32)
+            mine.append((jax.nn.silu(both[0]) * both[1]).astype(jnp.bfloat16))
+        mine = jnp.concatenate(mine, axis=1)
         other = flip(mine, "depth", 2)
         mine_passed = flip(mine, "depth", 1)
         other_passed = flip(other, "depth", 1)
         kinds = [jnp.bfloat16 if s else jnp.float32 for s in chunk]
-        outs = down(me, (mine, other, mine_passed, other_passed), down_weight, block_rows, kinds)
+        adds = [relayed[s] for s in chunk if s in relayed]
+        outs = down(me, (mine, other, mine_passed, other_passed), down_weight, block_rows, kinds, adds)
         for s, out in zip(chunk, outs):
-            if s:
-                arrived.append(flip(out, "grid", s))
+            if s == 0:
+                total = out
             else:
-                total = out
+                if number == FAR:
+                    relayed[s ^ per] = flip(out, "grid", per)
+                else:
+                    arrived.append(flip(out, "grid", s))
     for value in arrived:
         total = total + value.astype(jnp.float32)
     return total.astype(jnp.bfloat16)

time: 79.7 us -> 75.4 us (0.946)
  waiting for transfers between devices: 33.1 us -> 26.2 us
  starting transfers between devices: 23 us -> 26.2 us
  local copies, waits for them, and re-layouts: 6.07 us -> 4.18 us
  Pallas kernels: 15.8 us -> 17 us
    ppermute x26 -> x28, waiting for transfers between devices: 33.1 us -> 26.2 us  [flip(): return lax.ppermute(value, axis, [(i, i ^ bits) for i in range(size)])]
    ppermute x26 -> x28, starting transfers between devices: 23 us -> 26.2 us  [flip(): return lax.ppermute(value, axis, [(i, i ^ bits) for i in range(size)])]
    unnamed x10 -> x8, local copies, waits for them, and re-layouts: 6.07 us -> 4.18 us
    pallas_call x1, Pallas kernels: 0.01 us -> 1.06 us  [sort(): pl.pallas_call(sort_kernel, in_specs=[SMEM] + [VMEM] * len(xs), out_specs...]
    pallas_call x8 -> x9, Pallas kernels: 15.8 us -> 15.9 us  [the longest x5 10.4 us: up_gate(): pl.pallas_call(functools.partial(up_gate_kernel, blocks=len(xs), first=pi...]
  transfers between devices with their start and end apart: 26 -> 28, of which waited for: 10 -> 8; matrix products, arithmetic and copies ran while one was open for 1% -> 1% of each run, Pallas kernels for 17% -> 23%
where the time goes in v2:
time: 75.4 us; the launch traced here: 75.2 us
  starting transfers between devices  26.2 us (35%)
  waiting for transfers between devices  26.2 us (35%)
  Pallas kernels  17 us (23%)
  local copies, waits for them, and re-layouts  4.18 us (6%)
  other arithmetic  1.44 us (2%)
    ppermute x28, starting transfers between devices, flip(): return lax.ppermute(value, axis, [(i, i ^ bits) for i in range(size)])  26.2 us
    ppermute x28, waiting for transfers between devices, flip(): return lax.ppermute(value, axis, [(i, i ^ bits) for i in range(size)])  26.2 us
    pallas_call x5, Pallas kernels, up_gate(): pl.pallas_call(functools.partial(up_gate_kernel, blocks=len(xs), first=pi...  10.4 us
    pallas_call x4, Pallas kernels, down(): pl.pallas_call(functools.partial(down_kernel, blocks=len(kinds)), in_spec...  5.52 us
    unnamed x8, local copies, waits for them, and re-layouts  4.18 us
  transfers between devices with their start and end apart: 28, of which 8 were waited for; matrix products, arithmetic and copies ran while one was open for 1% of the time, Pallas kernels for 23%

profile of v2, /device:TPU:0, one launch (start us, length us, event | category | flops | bytes accessed | tf_op | source)
XLA Modules:
  0.0 75.2 jit_solution(12609460429505993762)
XLA Ops:
  0.0 4.1 %collective-permute-start.14 = (bf16[64,1024]{1,0:T(8,128)(2,1)}, bf16[64,1024]{1,0:T(8,128)(2,1)S(1)}, u32[]{:S(2)}, u32[]{:S(2)}) collective-permute-start(bf16[64,1024]{1,0:T(8,128)(2,1)} %refs_0_.1), channel_id=1, source_target_pairs={{0,8},{4,12},{8,0},{12,4},{1,9},{5,13},{9,1},{13,5},{2,10},{6,14},... | collective-permute-start | bytes 393224 | tf_op jit(solution)/shard_map/ppermute | solution.py:22
  4.1 1.3 %collective-permute-start.20 = (bf16[64,1024]{1,0:T(8,128)(2,1)}, bf16[64,1024]{1,0:T(8,128)(2,1)S(1)}, u32[]{:S(2)}, u32[]{:S(2)}) collective-permute-start(bf16[64,1024]{1,0:T(8,128)(2,1)} %refs_0_.1), channel_id=1, source_target_pairs={{0,12},{4,8},{8,4},{12,0},{1,13},{5,9},{9,5},{13,1},{2,14},{6,10},... | collective-permute-start | bytes 393224 | tf_op jit(solution)/shard_map/ppermute | solution.py:22
  5.7 1.1 %sort.1.refs_0_ = bf16[64,1024]{1,0:T(8,128)(2,1)S(1)} custom-call(s32[1]{0:T(128)} %bitcast.me_ref, bf16[64,1024]{1,0:T(8,128)(2,1)} %refs_0_.1), custom_call_target="tpu_custom_call" | custom-call | flops 10000000000 | tf_op jit(solution)/shard_map/sort/pallas_call | solution.py:47
  6.7 2.1 %copy-done = bf16[1024,3584]{1,0:T(8,128)(2,1)S(1)} copy-done((bf16[1024,3584]{1,0:T(8,128)(2,1)S(1)}, bf16[1024,3584]{1,0:T(8,128)(2,1)}, u32[]{:S(2)}) %copy-start) | copy-done | bytes 7340056
  8.8 2.1 %copy-done.1 = bf16[1024,3584]{1,0:T(8,128)(2,1)S(1)} copy-done((bf16[1024,3584]{1,0:T(8,128)(2,1)S(1)}, bf16[1024,3584]{1,0:T(8,128)(2,1)}, u32[]{:S(2)}) %copy-start.1) | copy-done | bytes 7340056
  10.9 1.3 %up_gate.6 = (bf16[2,32,1792]{2,1,0:T(8,128)(2,1)S(1)}, f32[2,32,1792]{2,1,0:T(8,128)S(1)}) custom-call(s32[1]{0:T(128)} %bitcast.me_ref, bf16[64,1024]{1,0:T(8,128)(2,1)S(1)} %sort.1.refs_0_, bf16[1024,3584]{1,0:T(8,128)(2,1)S(1)} %copy-done, bf16[1024,3584]{1,0:T(8,128)(2,1)S(1)} %copy-done.1), custom_call_target="tpu_custom_call" | custom-call | flops 469762048 | bytes 7340032 | tf_op jit(solution)/shard_map/up_gate/pallas_call | solution.py:78
  12.3 1.3 %up_gate.5 = (bf16[2,32,1792]{2,1,0:T(8,128)(2,1)S(1)}, f32[2,32,1792]{2,1,0:T(8,128)S(1)}) custom-call(s32[1]{0:T(128)} %bitcast.me_ref, bf16[64,1024]{1,0:T(8,128)(2,1)S(1)} %sort.1.refs_0_, bf16[1024,3584]{1,0:T(8,128)(2,1)S(1)} %copy-done, bf16[1024,3584]{1,0:T(8,128)(2,1)S(1)} %copy-done.1), custom_call_target="tpu_custom_call" | custom-call | flops 469762048 | bytes 7340032 | tf_op jit(solution)/shard_map/up_gate/pallas_call | solution.py:78
  13.7 0.6 collective-permute-start
  14.3 2.6 %up_gate.8 = (bf16[2,32,3584]{2,1,0:T(8,128)(2,1)S(1)}, f32[2,32,3584]{2,1,0:T(8,128)S(1)}) custom-call(s32[1]{0:T(128)} %bitcast.me_ref, bf16[64,1024]{1,0:T(8,128)(2,1)S(1)} %collective-permute-done.14.refs_0_, bf16[1024,3584]{1,0:T(8,128)(2,1)S(1)} %copy-done, bf16[1024,3584]{1,0:T(8,128)(2,1)S(1)} %copy-done.1), custom_call_target="tpu_custom_call" | custom-call | flops 939524096 | bytes 14680064 | tf_op jit(solution)/shard_map/up_gate/pallas_call | solution.py:78
  17.0 2.6 %up_gate.9 = (bf16[2,32,3584]{2,1,0:T(8,128)(2,1)S(1)}, f32[2,32,3584]{2,1,0:T(8,128)S(1)}) custom-call(s32[1]{0:T(128)} %bitcast.me_ref, bf16[64,1024]{1,0:T(8,128)(2,1)S(1)} %collective-permute-done.20.refs_0_, bf16[1024,3584]{1,0:T(8,128)(2,1)S(1)} %copy-done, bf16[1024,3584]{1,0:T(8,128)(2,1)S(1)} %copy-done.1), custom_call_target="tpu_custom_call" | custom-call | flops 939524096 | bytes 14680064 | tf_op jit(solution)/shard_map/up_gate/pallas_call | solution.py:78
  20.1 2.6 %up_gate.7 = (bf16[2,32,3584]{2,1,0:T(8,128)(2,1)S(1)}, f32[2,32,3584]{2,1,0:T(8,128)S(1)}) custom-call(s32[1]{0:T(128)} %bitcast.me_ref, bf16[64,1024]{1,0:T(8,128)(2,1)S(1)} %collective-permute-done.7.refs_0_, bf16[1024,3584]{1,0:T(8,128)(2,1)S(1)} %copy-done, bf16[1024,3584]{1,0:T(8,128)(2,1)S(1)} %copy-done.1), custom_call_target="tpu_custom_call" | custom-call | flops 939524096 | bytes 14680064 | tf_op jit(solution)/shard_map/up_gate/pallas_call | solution.py:78
  22.8 1.9 %collective-permute-start.3 = (bf16[2,16,1792]{2,1,0:T(8,128)(2,1)S(1)}, bf16[2,16,1792]{2,1,0:T(8,128)(2,1)S(1)}, u32[]{:S(2)}, u32[]{:S(2)}) collective-permute-start(bf16[2,16,1792]{2,1,0:T(8,128)(2,1)S(1)} %add_convert_fusion.4), channel_id=1, source_target_pairs={{0,2},{1,3},{2,0},{3,1},{4,6},{5,7},{6,4},{7,5},{8,10},{9,11},{10,... | collective-permute-start | bytes 344072 | tf_op jit(solution)/shard_map/ppermute | solution.py:22
  25.0 3.9 %collective-permute-done.3 = bf16[2,16,1792]{2,1,0:T(8,128)(2,1)S(1)} collective-permute-done((bf16[2,16,1792]{2,1,0:T(8,128)(2,1)S(1)}, bf16[2,16,1792]{2,1,0:T(8,128)(2,1)S(1)}, u32[]{:S(2)}, u32[]{:S(2)}) %collective-permute-start.3) | collective-permute-done | bytes 114720 | tf_op jit(solution)/shard_map/ppermute | solution.py:22
  29.0 2.0 %collective-permute-done.1 = bf16[2,16,1792]{2,1,0:T(8,128)(2,1)S(1)} collective-permute-done((bf16[2,16,1792]{2,1,0:T(8,128)(2,1)S(1)}, bf16[2,16,1792]{2,1,0:T(8,128)(2,1)S(1)}, u32[]{:S(2)}, u32[]{:S(2)}) %collective-permute-start.1) | collective-permute-done | bytes 114720 | tf_op jit(solution)/shard_map/ppermute | solution.py:22
  31.0 1.8 %collective-permute-start.4 = (bf16[16,3584]{1,0:T(8,128)(2,1)S(1)}, bf16[16,3584]{1,0:T(8,128)(2,1)S(1)}, u32[]{:S(2)}, u32[]{:S(2)}) collective-permute-start(bf16[16,3584]{1,0:T(8,128)(2,1)S(1)} %pad_maximum_fusion.h0), channel_id=1, source_target_pairs={{0,2},{1,3},{2,0},{3,1},{4,6},{5,7},{6,4},{7,5},{8,10},{9,11},{10,... | collective-permute-start | bytes 344072 | tf_op jit(solution)/shard_map/ppermute | solution.py:22
  33.3 1.8 %collective-permute-start.22 = (bf16[2,16,3584]{2,1,0:T(8,128)(2,1)S(1)}, bf16[2,16,3584]{2,1,0:T(8,128)(2,1)S(1)}, u32[]{:S(2)}, u32[]{:S(2)}) collective-permute-start(bf16[2,16,3584]{2,1,0:T(8,128)(2,1)S(1)} %add_convert_fusion), channel_id=1, source_target_pairs={{0,2},{1,3},{2,0},{3,1},{4,6},{5,7},{6,4},{7,5},{8,10},{9,11},{10,... | collective-permute-start | bytes 688136 | tf_op jit(solution)/shard_map/ppermute | solution.py:22
  35.5 11.2 %collective-permute-done.22 = bf16[2,16,3584]{2,1,0:T(8,128)(2,1)S(1)} collective-permute-done((bf16[2,16,3584]{2,1,0:T(8,128)(2,1)S(1)}, bf16[2,16,3584]{2,1,0:T(8,128)(2,1)S(1)}, u32[]{:S(2)}, u32[]{:S(2)}) %collective-permute-start.22) | collective-permute-done | bytes 229408 | tf_op jit(solution)/shard_map/ppermute | solution.py:22
  46.9 2.0 %collective-permute-start.23 = (bf16[16,3584]{1,0:T(8,128)(2,1)S(1)}, bf16[16,3584]{1,0:T(8,128)(2,1)S(1)}, u32[]{:S(2)}, u32[]{:S(2)}) collective-permute-start(bf16[16,3584]{1,0:T(8,128)(2,1)S(1)} %fusion.1.h0), channel_id=1, source_target_pairs={{0,2},{1,3},{2,0},{3,1},{4,6},{5,7},{6,4},{7,5},{8,10},{9,11},{10,... | collective-permute-start | bytes 344072 | tf_op jit(solution)/shard_map/ppermute | solution.py:22
  48.9 2.7 %collective-permute-done.9 = bf16[2,16,3584]{2,1,0:T(8,128)(2,1)S(1)} collective-permute-done((bf16[2,16,3584]{2,1,0:T(8,128)(2,1)S(1)}, bf16[2,16,3584]{2,1,0:T(8,128)(2,1)S(1)}, u32[]{:S(2)}, u32[]{:S(2)}) %collective-permute-start.9) | collective-permute-done | bytes 229408 | tf_op jit(solution)/shard_map/ppermute | solution.py:22
  51.8 1.9 %collective-permute-start.10 = (bf16[16,3584]{1,0:T(8,128)(2,1)S(1)}, bf16[16,3584]{1,0:T(8,128)(2,1)S(1)}, u32[]{:S(2)}, u32[]{:S(2)}) collective-permute-start(bf16[16,3584]{1,0:T(8,128)(2,1)S(1)} %fusion.5.h0), channel_id=1, source_target_pairs={{0,2},{1,3},{2,0},{3,1},{4,6},{5,7},{6,4},{7,5},{8,10},{9,11},{10,... | collective-permute-start | bytes 344072 | tf_op jit(solution)/shard_map/ppermute | solution.py:22
  54.0 1.8 %collective-permute-start.17 = (bf16[16,3584]{1,0:T(8,128)(2,1)S(1)}, bf16[16,3584]{1,0:T(8,128)(2,1)S(1)}, u32[]{:S(2)}, u32[]{:S(2)}) collective-permute-start(bf16[16,3584]{1,0:T(8,128)(2,1)S(1)} %fusion.3.h0), channel_id=1, source_target_pairs={{0,2},{1,3},{2,0},{3,1},{4,6},{5,7},{6,4},{7,5},{8,10},{9,11},{10,... | collective-permute-start | bytes 344072 | tf_op jit(solution)/shard_map/ppermute | solution.py:22
  56.0 0.7 collective-permute-done.10.h2
  56.7 1.4 %down.6 = bf16[64,1024]{1,0:T(8,128)(2,1)S(1)} custom-call(s32[1]{0:T(128)} %bitcast.me_ref, bf16[16,3584]{1,0:T(8,128)(2,1)S(1)} %fusion.1.h0, bf16[16,3584]{1,0:T(8,128)(2,1)S(1)} %collective-permute-done.23.h2, bf16[16,3584]{1,0:T(8,128)(2,1)S(1)} %collective-permute-done.24.h1, bf16[16,3584]{1,0:T(8,128)(2,1)S(1)} %collective-permute-done.25.h3, ...), custom_call_target="tpu_custom_call" | custom-call | flops 469762048 | bytes 7340032 | tf_op jit(solution)/shard_map/down/pallas_call | solution.py:118
  58.1 1.9 %collective-permute-start.26 = (bf16[64,1024]{1,0:T(8,128)(2,1)S(1)}, bf16[64,1024]{1,0:T(8,128)(2,1)S(1)}, u32[]{:S(2)}, u32[]{:S(2)}) collective-permute-start(bf16[64,1024]{1,0:T(8,128)(2,1)S(1)} %down.6), channel_id=1, source_target_pairs={{0,4},{4,0},{8,12},{12,8},{1,5},{5,1},{9,13},{13,9},{2,6},{6,2},{1... | collective-permute-start | bytes 393224 | tf_op jit(solution)/shard_map/ppermute | solution.py:22
  61.1 1.4 %down.5 = bf16[64,1024]{1,0:T(8,128)(2,1)S(1)} custom-call(s32[1]{0:T(128)} %bitcast.me_ref, bf16[16,3584]{1,0:T(8,128)(2,1)S(1)} %fusion.5.h0, bf16[16,3584]{1,0:T(8,128)(2,1)S(1)} %collective-permute-done.10.h2, bf16[16,3584]{1,0:T(8,128)(2,1)S(1)} %collective-permute-done.11.h1, bf16[16,3584]{1,0:T(8,128)(2,1)S(1)} %collective-permute-done.12.h3, ...), custom_call_target="tpu_custom_call" | custom-call | flops 469762048 | bytes 7340032 | tf_op jit(solution)/shard_map/down/pallas_call | solution.py:118
  62.5 0.9 %collective-permute-start.13 = (bf16[64,1024]{1,0:T(8,128)(2,1)S(1)}, bf16[64,1024]{1,0:T(8,128)(2,1)S(1)}, u32[]{:S(2)}, u32[]{:S(2)}) collective-permute-start(bf16[64,1024]{1,0:T(8,128)(2,1)S(1)} %down.5), channel_id=1, source_target_pairs={{0,4},{4,0},{8,12},{12,8},{1,5},{5,1},{9,13},{13,9},{2,6},{6,2},{1... | collective-permute-start | bytes 393224 | tf_op jit(solution)/shard_map/ppermute | solution.py:22
  63.3 0.9 %collective-permute-done.26.refs_0_ = bf16[64,1024]{1,0:T(8,128)(2,1)S(1)} collective-permute-done((bf16[64,1024]{1,0:T(8,128)(2,1)S(1)}, bf16[64,1024]{1,0:T(8,128)(2,1)S(1)}, u32[]{:S(2)}, u32[]{:S(2)}) %collective-permute-start.26) | collective-permute-done | bytes 131104 | tf_op jit(solution)/shard_map/ppermute | solution.py:22
  64.2 1.4 %down.7 = bf16[64,1024]{1,0:T(8,128)(2,1)S(1)} custom-call(s32[1]{0:T(128)} %bitcast.me_ref, bf16[16,3584]{1,0:T(8,128)(2,1)S(1)} %fusion.3.h0, bf16[16,3584]{1,0:T(8,128)(2,1)S(1)} %collective-permute-done.17.h2, bf16[16,3584]{1,0:T(8,128)(2,1)S(1)} %collective-permute-done.18.h1, bf16[16,3584]{1,0:T(8,128)(2,1)S(1)} %collective-permute-done.19.h3, ...), custom_call_target="tpu_custom_call" | custom-call | flops 469762048 | bytes 7340032 | tf_op jit(solution)/shard_map/down/pallas_call | solution.py:118
  65.6 2.8 %collective-permute-start.27 = (bf16[64,1024]{1,0:T(8,128)(2,1)S(1)}, bf16[64,1024]{1,0:T(8,128)(2,1)S(1)}, u32[]{:S(2)}, u32[]{:S(2)}) collective-permute-start(bf16[64,1024]{1,0:T(8,128)(2,1)S(1)} %down.7), channel_id=1, source_target_pairs={{0,8},{4,12},{8,0},{12,4},{1,9},{5,13},{9,1},{13,5},{2,10},{6,14},... | collective-permute-start | bytes 393224 | tf_op jit(solution)/shard_map/ppermute | solution.py:22
  68.4 1.4 %down.4 = f32[64,1024]{1,0:T(8,128)S(1)} custom-call(s32[1]{0:T(128)} %bitcast.me_ref, bf16[16,3584]{1,0:T(8,128)(2,1)S(1)} %pad_maximum_fusion.h0, bf16[16,3584]{1,0:T(8,128)(2,1)S(1)} %collective-permute-done.4.h2, bf16[16,3584]{1,0:T(8,128)(2,1)S(1)} %collective-permute-done.5.h1, bf16[16,3584]{1,0:T(8,128)(2,1)S(1)} %collective-permute-done.6.h3, ...), custom_call_target="tpu_custom_call" | custom-call | flops 469762048 | bytes 7340032 | tf_op jit(solution)/shard_map/down/pallas_call | solution.py:118
  69.8 4.7 %collective-permute-done.27 = bf16[64,1024]{1,0:T(8,128)(2,1)S(1)} collective-permute-done((bf16[64,1024]{1,0:T(8,128)(2,1)S(1)}, bf16[64,1024]{1,0:T(8,128)(2,1)S(1)}, u32[]{:S(2)}, u32[]{:S(2)}) %collective-permute-start.27) | collective-permute-done | bytes 131104 | tf_op jit(solution)/shard_map/ppermute | solution.py:22
  74.5 0.7 add_convert_fusion.3
  (60 shorter events, 4.2 us)
Async XLA Ops:
  0.0 14.3 %collective-permute-start.14 = (bf16[64,1024]{1,0:T(8,128)(2,1)}, bf16[64,1024]{1,0:T(8,128)(2,1)S(1)}, u32[]{:S(2)}, u32[]{:S(2)}) collective-permute-start(bf16[64,1024]{1,0:T(8,128)(2,1)} %refs_0_.1), channel_id=1, source_target_pairs={{0,8},{4,12},{8,0},{12,4},{1,9},{5,13},{9,1},{13,5},{2,10},{6,14},... | collective-permute-start | bytes 393224 | tf_op jit(solution)/shard_map/ppermute | solution.py:22
  4.1 12.9 %collective-permute-start.20 = (bf16[64,1024]{1,0:T(8,128)(2,1)}, bf16[64,1024]{1,0:T(8,128)(2,1)S(1)}, u32[]{:S(2)}, u32[]{:S(2)}) collective-permute-start(bf16[64,1024]{1,0:T(8,128)(2,1)} %refs_0_.1), channel_id=1, source_target_pairs={{0,12},{4,8},{8,4},{12,0},{1,13},{5,9},{9,5},{13,1},{2,14},{6,10},... | collective-permute-start | bytes 393224 | tf_op jit(solution)/shard_map/ppermute | solution.py:22
  5.4 14.7 %collective-permute-start.7 = (bf16[64,1024]{1,0:T(8,128)(2,1)}, bf16[64,1024]{1,0:T(8,128)(2,1)S(1)}, u32[]{:S(2)}, u32[]{:S(2)}) collective-permute-start(bf16[64,1024]{1,0:T(8,128)(2,1)} %refs_0_.1), channel_id=1, source_target_pairs={{0,4},{4,0},{8,12},{12,8},{1,5},{5,1},{9,13},{13,9},{2,6},{6,2},{1... | collective-permute-start | bytes 393224 | tf_op jit(solution)/shard_map/ppermute | solution.py:22
  5.6 3.1 %copy-start = (bf16[1024,3584]{1,0:T(8,128)(2,1)S(1)}, bf16[1024,3584]{1,0:T(8,128)(2,1)}, u32[]{:S(2)}) copy-start(bf16[1024,3584]{1,0:T(8,128)(2,1)} %refs_1_.9) | copy-start | bytes 22020100
  5.6 5.2 %copy-start.1 = (bf16[1024,3584]{1,0:T(8,128)(2,1)S(1)}, bf16[1024,3584]{1,0:T(8,128)(2,1)}, u32[]{:S(2)}) copy-start(bf16[1024,3584]{1,0:T(8,128)(2,1)} %refs_2_.9) | copy-start | bytes 22020100
  12.2 10.6 %collective-permute-start.2 = (bf16[2,32,1792]{2,1,0:T(8,128)(2,1)S(1)}, bf16[2,32,1792]{2,1,0:T(8,128)(2,1)S(1)}, u32[]{:S(2)}, u32[]{:S(2)}) collective-permute-start(bf16[2,32,1792]{2,1,0:T(8,128)(2,1)S(1)} %get-tuple-element.18), channel_id=1, source_target_pairs={{0,1},{1,0},{2,3},{3,2},{4,5},{5,4},{6,7},{7,6},{8,9},{9,8},{10,11... | collective-permute-start | bytes 688136 | tf_op jit(solution)/shard_map/ppermute | solution.py:22
  13.7 11.0 %collective-permute-start = (bf16[2,32,1792]{2,1,0:T(8,128)(2,1)S(1)}, bf16[2,32,1792]{2,1,0:T(8,128)(2,1)S(1)}, u32[]{:S(2)}, u32[]{:S(2)}) collective-permute-start(bf16[2,32,1792]{2,1,0:T(8,128)(2,1)S(1)} %get-tuple-element.16), channel_id=1, source_target_pairs={{0,1},{1,0},{2,3},{3,2},{4,5},{5,4},{6,7},{7,6},{8,9},{9,8},{10,11... | collective-permute-start | bytes 688136 | tf_op jit(solution)/shard_map/ppermute | solution.py:22
  16.9 16.0 %collective-permute-start.15 = (bf16[2,32,3584]{2,1,0:T(8,128)(2,1)S(1)}, bf16[2,32,3584]{2,1,0:T(8,128)(2,1)S(1)}, u32[]{:S(2)}, u32[]{:S(2)}) collective-permute-start(bf16[2,32,3584]{2,1,0:T(8,128)(2,1)S(1)} %get-tuple-element.22), channel_id=1, source_target_pairs={{0,1},{1,0},{2,3},{3,2},{4,5},{5,4},{6,7},{7,6},{8,9},{9,8},{10,11... | collective-permute-start | bytes 1376264 | tf_op jit(solution)/shard_map/ppermute | solution.py:22
  19.5 37.1 %slice-start = ((s8[7340032]{0:T(1024)(128)(4,1)}), s8[4194304]{0:T(1024)(128)(4,1)S(1)}, s32[]{:S(2)}) async-start(s8[7340032]{0:T(1024)(128)(4,1)} %bitcast.51), calls=%async_computation | async-start | bytes 8388608
  19.6 37.1 %slice-start.1 = ((s8[7340032]{0:T(1024)(128)(4,1)}), s8[3145728]{0:T(1024)(128)(4,1)S(1)}, s32[]{:S(2)}) async-start(s8[7340032]{0:T(1024)(128)(4,1)} %bitcast.51), calls=%async_computation.1 | async-start | bytes 6291456
  19.6 13.7 %collective-permute-start.21 = (bf16[2,32,3584]{2,1,0:T(8,128)(2,1)S(1)}, bf16[2,32,3584]{2,1,0:T(8,128)(2,1)S(1)}, u32[]{:S(2)}, u32[]{:S(2)}) collective-permute-start(bf16[2,32,3584]{2,1,0:T(8,128)(2,1)S(1)} %get-tuple-element.24), channel_id=1, source_target_pairs={{0,1},{1,0},{2,3},{3,2},{4,5},{5,4},{6,7},{7,6},{8,9},{9,8},{10,11... | collective-permute-start | bytes 1376264 | tf_op jit(solution)/shard_map/ppermute | solution.py:22
  22.7 12.4 %collective-permute-start.8 = (bf16[2,32,3584]{2,1,0:T(8,128)(2,1)S(1)}, bf16[2,32,3584]{2,1,0:T(8,128)(2,1)S(1)}, u32[]{:S(2)}, u32[]{:S(2)}) collective-permute-start(bf16[2,32,3584]{2,1,0:T(8,128)(2,1)S(1)} %get-tuple-element.20), channel_id=1, source_target_pairs={{0,1},{1,0},{2,3},{3,2},{4,5},{5,4},{6,7},{7,6},{8,9},{9,8},{10,11... | collective-permute-start | bytes 1376264 | tf_op jit(solution)/shard_map/ppermute | solution.py:22
  22.8 6.1 %collective-permute-start.3 = (bf16[2,16,1792]{2,1,0:T(8,128)(2,1)S(1)}, bf16[2,16,1792]{2,1,0:T(8,128)(2,1)S(1)}, u32[]{:S(2)}, u32[]{:S(2)}) collective-permute-start(bf16[2,16,1792]{2,1,0:T(8,128)(2,1)S(1)} %add_convert_fusion.4), channel_id=1, source_target_pairs={{0,2},{1,3},{2,0},{3,1},{4,6},{5,7},{6,4},{7,5},{8,10},{9,11},{10,... | collective-permute-start | bytes 344072 | tf_op jit(solution)/shard_map/ppermute | solution.py:22
  24.7 6.2 %collective-permute-start.1 = (bf16[2,16,1792]{2,1,0:T(8,128)(2,1)S(1)}, bf16[2,16,1792]{2,1,0:T(8,128)(2,1)S(1)}, u32[]{:S(2)}, u32[]{:S(2)}) collective-permute-start(bf16[2,16,1792]{2,1,0:T(8,128)(2,1)S(1)} %add_convert_fusion.5), channel_id=1, source_target_pairs={{0,2},{1,3},{2,0},{3,1},{4,6},{5,7},{6,4},{7,5},{8,10},{9,11},{10,... | collective-permute-start | bytes 344072 | tf_op jit(solution)/shard_map/ppermute | solution.py:22
  31.0 29.0 %collective-permute-start.4 = (bf16[16,3584]{1,0:T(8,128)(2,1)S(1)}, bf16[16,3584]{1,0:T(8,128)(2,1)S(1)}, u32[]{:S(2)}, u32[]{:S(2)}) collective-permute-start(bf16[16,3584]{1,0:T(8,128)(2,1)S(1)} %pad_maximum_fusion.h0), channel_id=1, source_target_pairs={{0,2},{1,3},{2,0},{3,1},{4,6},{5,7},{6,4},{7,5},{8,10},{9,11},{10,... | collective-permute-start | bytes 344072 | tf_op jit(solution)/shard_map/ppermute | solution.py:22
  32.9 20.8 %collective-permute-start.16 = (bf16[2,16,3584]{2,1,0:T(8,128)(2,1)S(1)}, bf16[2,16,3584]{2,1,0:T(8,128)(2,1)S(1)}, u32[]{:S(2)}, u32[]{:S(2)}) collective-permute-start(bf16[2,16,3584]{2,1,0:T(8,128)(2,1)S(1)} %add_convert_fusion.1), channel_id=1, source_target_pairs={{0,2},{1,3},{2,0},{3,1},{4,6},{5,7},{6,4},{7,5},{8,10},{9,11},{10,... | collective-permute-start | bytes 688136 | tf_op jit(solution)/shard_map/ppermute | solution.py:22
  33.3 13.4 %collective-permute-start.22 = (bf16[2,16,3584]{2,1,0:T(8,128)(2,1)S(1)}, bf16[2,16,3584]{2,1,0:T(8,128)(2,1)S(1)}, u32[]{:S(2)}, u32[]{:S(2)}) collective-permute-start(bf16[2,16,3584]{2,1,0:T(8,128)(2,1)S(1)} %add_convert_fusion), channel_id=1, source_target_pairs={{0,2},{1,3},{2,0},{3,1},{4,6},{5,7},{6,4},{7,5},{8,10},{9,11},{10,... | collective-permute-start | bytes 688136 | tf_op jit(solution)/shard_map/ppermute | solution.py:22
  35.2 16.5 %collective-permute-start.9 = (bf16[2,16,3584]{2,1,0:T(8,128)(2,1)S(1)}, bf16[2,16,3584]{2,1,0:T(8,128)(2,1)S(1)}, u32[]{:S(2)}, u32[]{:S(2)}) collective-permute-start(bf16[2,16,3584]{2,1,0:T(8,128)(2,1)S(1)} %add_convert_fusion.2), channel_id=1, source_target_pairs={{0,2},{1,3},{2,0},{3,1},{4,6},{5,7},{6,4},{7,5},{8,10},{9,11},{10,... | collective-permute-start | bytes 688136 | tf_op jit(solution)/shard_map/ppermute | solution.py:22
  46.9 6.9 %collective-permute-start.23 = (bf16[16,3584]{1,0:T(8,128)(2,1)S(1)}, bf16[16,3584]{1,0:T(8,128)(2,1)S(1)}, u32[]{:S(2)}, u32[]{:S(2)}) collective-permute-start(bf16[16,3584]{1,0:T(8,128)(2,1)S(1)} %fusion.1.h0), channel_id=1, source_target_pairs={{0,2},{1,3},{2,0},{3,1},{4,6},{5,7},{6,4},{7,5},{8,10},{9,11},{10,... | collective-permute-start | bytes 344072 | tf_op jit(solution)/shard_map/ppermute | solution.py:22
  48.9 6.8 %collective-permute-start.24 = (bf16[16,3584]{1,0:T(8,128)(2,1)S(1)}, bf16[16,3584]{1,0:T(8,128)(2,1)S(1)}, u32[]{:S(2)}, u32[]{:S(2)}) collective-permute-start(bf16[16,3584]{1,0:T(8,128)(2,1)S(1)} %fusion.1.h0), channel_id=1, source_target_pairs={{0,1},{1,0},{2,3},{3,2},{4,5},{5,4},{6,7},{7,6},{8,9},{9,8},{10,11... | collective-permute-start | bytes 344072 | tf_op jit(solution)/shard_map/ppermute | solution.py:22
  51.8 4.9 %collective-permute-start.10 = (bf16[16,3584]{1,0:T(8,128)(2,1)S(1)}, bf16[16,3584]{1,0:T(8,128)(2,1)S(1)}, u32[]{:S(2)}, u32[]{:S(2)}) collective-permute-start(bf16[16,3584]{1,0:T(8,128)(2,1)S(1)} %fusion.5.h0), channel_id=1, source_target_pairs={{0,2},{1,3},{2,0},{3,1},{4,6},{5,7},{6,4},{7,5},{8,10},{9,11},{10,... | collective-permute-start | bytes 344072 | tf_op jit(solution)/shard_map/ppermute | solution.py:22
  53.8 2.9 %collective-permute-start.25 = (bf16[16,3584]{1,0:T(8,128)(2,1)S(1)}, bf16[16,3584]{1,0:T(8,128)(2,1)S(1)}, u32[]{:S(2)}, u32[]{:S(2)}) collective-permute-start(bf16[16,3584]{1,0:T(8,128)(2,1)S(1)} %collective-permute-done.23.h2), channel_id=1, source_target_pairs={{0,1},{1,0},{2,3},{3,2},{4,5},{5,4},{6,7},{7,6},{8,9},{9,8},{10,11... | collective-permute-start | bytes 344072 | tf_op jit(solution)/shard_map/ppermute | solution.py:22
  54.0 6.3 %collective-permute-start.17 = (bf16[16,3584]{1,0:T(8,128)(2,1)S(1)}, bf16[16,3584]{1,0:T(8,128)(2,1)S(1)}, u32[]{:S(2)}, u32[]{:S(2)}) collective-permute-start(bf16[16,3584]{1,0:T(8,128)(2,1)S(1)} %fusion.3.h0), channel_id=1, source_target_pairs={{0,2},{1,3},{2,0},{3,1},{4,6},{5,7},{6,4},{7,5},{8,10},{9,11},{10,... | collective-permute-start | bytes 344072 | tf_op jit(solution)/shard_map/ppermute | solution.py:22
  55.8 4.8 %collective-permute-start.11 = (bf16[16,3584]{1,0:T(8,128)(2,1)S(1)}, bf16[16,3584]{1,0:T(8,128)(2,1)S(1)}, u32[]{:S(2)}, u32[]{:S(2)}) collective-permute-start(bf16[16,3584]{1,0:T(8,128)(2,1)S(1)} %fusion.5.h0), channel_id=1, source_target_pairs={{0,1},{1,0},{2,3},{3,2},{4,5},{5,4},{6,7},{7,6},{8,9},{9,8},{10,11... | collective-permute-start | bytes 344072 | tf_op jit(solution)/shard_map/ppermute | solution.py:22
  56.7 4.1 %collective-permute-start.12 = (bf16[16,3584]{1,0:T(8,128)(2,1)S(1)}, bf16[16,3584]{1,0:T(8,128)(2,1)S(1)}, u32[]{:S(2)}, u32[]{:S(2)}) collective-permute-start(bf16[16,3584]{1,0:T(8,128)(2,1)S(1)} %collective-permute-done.10.h2), channel_id=1, source_target_pairs={{0,1},{1,0},{2,3},{3,2},{4,5},{5,4},{6,7},{7,6},{8,9},{9,8},{10,11... | collective-permute-start | bytes 344072 | tf_op jit(solution)/shard_map/ppermute | solution.py:22
  58.1 6.1 %collective-permute-start.26 = (bf16[64,1024]{1,0:T(8,128)(2,1)S(1)}, bf16[64,1024]{1,0:T(8,128)(2,1)S(1)}, u32[]{:S(2)}, u32[]{:S(2)}) collective-permute-start(bf16[64,1024]{1,0:T(8,128)(2,1)S(1)} %down.6), channel_id=1, source_target_pairs={{0,4},{4,0},{8,12},{12,8},{1,5},{5,1},{9,13},{13,9},{2,6},{6,2},{1... | collective-permute-start | bytes 393224 | tf_op jit(solution)/shard_map/ppermute | solution.py:22
  60.0 2.4 %collective-permute-start.18 = (bf16[16,3584]{1,0:T(8,128)(2,1)S(1)}, bf16[16,3584]{1,0:T(8,128)(2,1)S(1)}, u32[]{:S(2)}, u32[]{:S(2)}) collective-permute-start(bf16[16,3584]{1,0:T(8,128)(2,1)S(1)} %fusion.3.h0), channel_id=1, source_target_pairs={{0,1},{1,0},{2,3},{3,2},{4,5},{5,4},{6,7},{7,6},{8,9},{9,8},{10,11... | collective-permute-start | bytes 344072 | tf_op jit(solution)/shard_map/ppermute | solution.py:22
  60.2 3.1 %collective-permute-start.19 = (bf16[16,3584]{1,0:T(8,128)(2,1)S(1)}, bf16[16,3584]{1,0:T(8,128)(2,1)S(1)}, u32[]{:S(2)}, u32[]{:S(2)}) collective-permute-start(bf16[16,3584]{1,0:T(8,128)(2,1)S(1)} %collective-permute-done.17.h2), channel_id=1, source_target_pairs={{0,1},{1,0},{2,3},{3,2},{4,5},{5,4},{6,7},{7,6},{8,9},{9,8},{10,11... | collective-permute-start | bytes 344072 | tf_op jit(solution)/shard_map/ppermute | solution.py:22
  60.5 7.9 %collective-permute-start.5 = (bf16[16,3584]{1,0:T(8,128)(2,1)S(1)}, bf16[16,3584]{1,0:T(8,128)(2,1)S(1)}, u32[]{:S(2)}, u32[]{:S(2)}) collective-permute-start(bf16[16,3584]{1,0:T(8,128)(2,1)S(1)} %pad_maximum_fusion.h0), channel_id=1, source_target_pairs={{0,1},{1,0},{2,3},{3,2},{4,5},{5,4},{6,7},{7,6},{8,9},{9,8},{10,11... | collective-permute-start | bytes 344072 | tf_op jit(solution)/shard_map/ppermute | solution.py:22
  60.8 7.6 %collective-permute-start.6 = (bf16[16,3584]{1,0:T(8,128)(2,1)S(1)}, bf16[16,3584]{1,0:T(8,128)(2,1)S(1)}, u32[]{:S(2)}, u32[]{:S(2)}) collective-permute-start(bf16[16,3584]{1,0:T(8,128)(2,1)S(1)} %collective-permute-done.4.h2), channel_id=1, source_target_pairs={{0,1},{1,0},{2,3},{3,2},{4,5},{5,4},{6,7},{7,6},{8,9},{9,8},{10,11... | collective-permute-start | bytes 344072 | tf_op jit(solution)/shard_map/ppermute | solution.py:22
  62.5 7.3 %collective-permute-start.13 = (bf16[64,1024]{1,0:T(8,128)(2,1)S(1)}, bf16[64,1024]{1,0:T(8,128)(2,1)S(1)}, u32[]{:S(2)}, u32[]{:S(2)}) collective-permute-start(bf16[64,1024]{1,0:T(8,128)(2,1)S(1)} %down.5), channel_id=1, source_target_pairs={{0,4},{4,0},{8,12},{12,8},{1,5},{5,1},{9,13},{13,9},{2,6},{6,2},{1... | collective-permute-start | bytes 393224 | tf_op jit(solution)/shard_map/ppermute | solution.py:22
  65.6 9.0 %collective-permute-start.27 = (bf16[64,1024]{1,0:T(8,128)(2,1)S(1)}, bf16[64,1024]{1,0:T(8,128)(2,1)S(1)}, u32[]{:S(2)}, u32[]{:S(2)}) collective-permute-start(bf16[64,1024]{1,0:T(8,128)(2,1)S(1)} %down.7), channel_id=1, source_target_pairs={{0,8},{4,12},{8,0},{12,4},{1,9},{5,13},{9,1},{13,5},{2,10},{6,14},... | collective-permute-start | bytes 393224 | tf_op jit(solution)/shard_map/ppermute | solution.py:22

commit v3 on v2

--- a/solution.py
+++ b/solution.py
@@ -27,7 +27,7 @@
 
 
 def width_of(hidden):
-    return next((w for w in (896, 512, 384, 256, 128) if hidden % w == 0), hidden)
+    return next((w for w in (1792, 896, 512, 384, 256, 128) if hidden % w == 0), hidden)
 
 
 def sort_rows(me, x_refs, x_sc):
@@ -61,6 +61,8 @@
         sort_rows(me_ref[0], x_refs, scratch[0])
     x = (scratch or x_refs)[0][...]
     half = x.shape[0] // 2
+    if x.shape[0] < 128:
+        x = jnp.concatenate([x, x], axis=0)
     share = send_ref.shape[2]
     width = width_of(share)
     for j in range(share // width):
@@ -69,7 +71,7 @@
         for i, w_ref in enumerate((g_ref, u_ref)):
             y = jnp.dot(x, w_ref[:, taken], preferred_element_type=jnp.float32)
             send_ref[i, :, cols] = y[:half].astype(send_ref.dtype)
-            keep_ref[i, :, cols] = y[half:]
+            keep_ref[i, :, cols] = y[half : 2 * half]
 
 
 def up_gate(me, xs, gate, up, ordered, piece, pieces):
@@ -96,6 +98,8 @@
     outs, adds = refs[-blocks:], refs[:-blocks]
     me = me_ref[0]
     h = jnp.concatenate([h0[...], h2[...], h1[...], h3[...]], axis=0)
+    if h.shape[0] < 128:
+        h = jnp.concatenate([h, h], axis=0)
     part = outs[0].shape[0] // len(ORDER)
     depth = w_ref.shape[1]
     width = 256 if depth % 256 == 0 else depth

time: 75.4 us -> 73.1 us (0.969)
  Pallas kernels: 17 us -> 14.2 us
  waiting for transfers between devices: 26.2 us -> 27.3 us
    pallas_call x5, Pallas kernels: 10.4 us -> 8.45 us  [up_gate(): pl.pallas_call(functools.partial(up_gate_kernel, blocks=len(xs), first=pi...]
    ppermute x28, waiting for transfers between devices: 26.2 us -> 27.3 us  [flip(): return lax.ppermute(value, axis, [(i, i ^ bits) for i in range(size)])]
    pallas_call x4, Pallas kernels: 5.52 us -> 4.72 us  [down(): pl.pallas_call(functools.partial(down_kernel, blocks=len(kinds)), in_spec...]
  transfers between devices with their start and end apart: 28 -> 28, of which waited for: 8 -> 8; matrix products, arithmetic and copies ran while one was open for 1% -> 1% of each run, Pallas kernels for 23% -> 20%
where the time goes in v3:
time: 73.1 us; the launch traced here: 72.9 us
  waiting for transfers between devices  27.3 us (37%)
  starting transfers between devices  25.5 us (35%)
  Pallas kernels  14.2 us (19%)
  local copies, waits for them, and re-layouts  4.18 us (6%)
  other arithmetic  1.44 us (2%)
    ppermute x28, waiting for transfers between devices, flip(): return lax.ppermute(value, axis, [(i, i ^ bits) for i in range(size)])  27.3 us
    ppermute x28, starting transfers between devices, flip(): return lax.ppermute(value, axis, [(i, i ^ bits) for i in range(size)])  25.5 us
    pallas_call x5, Pallas kernels, up_gate(): pl.pallas_call(functools.partial(up_gate_kernel, blocks=len(xs), first=pi...  8.45 us
    pallas_call x4, Pallas kernels, down(): pl.pallas_call(functools.partial(down_kernel, blocks=len(kinds)), in_spec...  4.72 us
    unnamed x8, local copies, waits for them, and re-layouts  4.18 us
  transfers between devices with their start and end apart: 28, of which 8 were waited for; matrix products, arithmetic and copies ran while one was open for 1% of the time, Pallas kernels for 20%

profile of v3, /device:TPU:0, one launch (start us, length us, event | category | flops | bytes accessed | tf_op | source)
XLA Modules:
  0.0 72.9 jit_solution(6413249291509480420)
XLA Ops:
  0.0 4.1 %collective-permute-start.14 = (bf16[64,1024]{1,0:T(8,128)(2,1)}, bf16[64,1024]{1,0:T(8,128)(2,1)S(1)}, u32[]{:S(2)}, u32[]{:S(2)}) collective-permute-start(bf16[64,1024]{1,0:T(8,128)(2,1)} %refs_0_.1), channel_id=1, source_target_pairs={{0,8},{4,12},{8,0},{12,4},{1,9},{5,13},{9,1},{13,5},{2,10},{6,14},... | collective-permute-start | bytes 393224 | tf_op jit(solution)/shard_map/ppermute | solution.py:22
  4.1 1.3 %collective-permute-start.20 = (bf16[64,1024]{1,0:T(8,128)(2,1)}, bf16[64,1024]{1,0:T(8,128)(2,1)S(1)}, u32[]{:S(2)}, u32[]{:S(2)}) collective-permute-start(bf16[64,1024]{1,0:T(8,128)(2,1)} %refs_0_.1), channel_id=1, source_target_pairs={{0,12},{4,8},{8,4},{12,0},{1,13},{5,9},{9,5},{13,1},{2,14},{6,10},... | collective-permute-start | bytes 393224 | tf_op jit(solution)/shard_map/ppermute | solution.py:22
  5.7 1.1 %sort.1.refs_0_ = bf16[64,1024]{1,0:T(8,128)(2,1)S(1)} custom-call(s32[1]{0:T(128)} %bitcast.me_ref, bf16[64,1024]{1,0:T(8,128)(2,1)} %refs_0_.1), custom_call_target="tpu_custom_call" | custom-call | flops 10000000000 | tf_op jit(solution)/shard_map/sort/pallas_call | solution.py:47
  6.7 2.1 %copy-done = bf16[1024,3584]{1,0:T(8,128)(2,1)S(1)} copy-done((bf16[1024,3584]{1,0:T(8,128)(2,1)S(1)}, bf16[1024,3584]{1,0:T(8,128)(2,1)}, u32[]{:S(2)}) %copy-start) | copy-done | bytes 7340056
  8.8 2.1 %copy-done.1 = bf16[1024,3584]{1,0:T(8,128)(2,1)S(1)} copy-done((bf16[1024,3584]{1,0:T(8,128)(2,1)S(1)}, bf16[1024,3584]{1,0:T(8,128)(2,1)}, u32[]{:S(2)}) %copy-start.1) | copy-done | bytes 7340056
  10.9 1.1 %up_gate.6 = (bf16[2,32,1792]{2,1,0:T(8,128)(2,1)S(1)}, f32[2,32,1792]{2,1,0:T(8,128)S(1)}) custom-call(s32[1]{0:T(128)} %bitcast.me_ref, bf16[64,1024]{1,0:T(8,128)(2,1)S(1)} %sort.1.refs_0_, bf16[1024,3584]{1,0:T(8,128)(2,1)S(1)} %copy-done, bf16[1024,3584]{1,0:T(8,128)(2,1)S(1)} %copy-done.1), custom_call_target="tpu_custom_call" | custom-call | flops 469762048 | bytes 7340032 | tf_op jit(solution)/shard_map/up_gate/pallas_call | solution.py:80
  12.1 1.1 %up_gate.5 = (bf16[2,32,1792]{2,1,0:T(8,128)(2,1)S(1)}, f32[2,32,1792]{2,1,0:T(8,128)S(1)}) custom-call(s32[1]{0:T(128)} %bitcast.me_ref, bf16[64,1024]{1,0:T(8,128)(2,1)S(1)} %sort.1.refs_0_, bf16[1024,3584]{1,0:T(8,128)(2,1)S(1)} %copy-done, bf16[1024,3584]{1,0:T(8,128)(2,1)S(1)} %copy-done.1), custom_call_target="tpu_custom_call" | custom-call | flops 469762048 | bytes 7340032 | tf_op jit(solution)/shard_map/up_gate/pallas_call | solution.py:80
  13.2 0.6 collective-permute-start
  14.3 2.1 %up_gate.8 = (bf16[2,32,3584]{2,1,0:T(8,128)(2,1)S(1)}, f32[2,32,3584]{2,1,0:T(8,128)S(1)}) custom-call(s32[1]{0:T(128)} %bitcast.me_ref, bf16[64,1024]{1,0:T(8,128)(2,1)S(1)} %collective-permute-done.14.refs_0_, bf16[1024,3584]{1,0:T(8,128)(2,1)S(1)} %copy-done, bf16[1024,3584]{1,0:T(8,128)(2,1)S(1)} %copy-done.1), custom_call_target="tpu_custom_call" | custom-call | flops 939524096 | bytes 14680064 | tf_op jit(solution)/shard_map/up_gate/pallas_call | solution.py:80
  16.5 2.1 %up_gate.9 = (bf16[2,32,3584]{2,1,0:T(8,128)(2,1)S(1)}, f32[2,32,3584]{2,1,0:T(8,128)S(1)}) custom-call(s32[1]{0:T(128)} %bitcast.me_ref, bf16[64,1024]{1,0:T(8,128)(2,1)S(1)} %collective-permute-done.20.refs_0_, bf16[1024,3584]{1,0:T(8,128)(2,1)S(1)} %copy-done, bf16[1024,3584]{1,0:T(8,128)(2,1)S(1)} %copy-done.1), custom_call_target="tpu_custom_call" | custom-call | flops 939524096 | bytes 14680064 | tf_op jit(solution)/shard_map/up_gate/pallas_call | solution.py:80
  19.1 2.1 %up_gate.7 = (bf16[2,32,3584]{2,1,0:T(8,128)(2,1)S(1)}, f32[2,32,3584]{2,1,0:T(8,128)S(1)}) custom-call(s32[1]{0:T(128)} %bitcast.me_ref, bf16[64,1024]{1,0:T(8,128)(2,1)S(1)} %collective-permute-done.7.refs_0_, bf16[1024,3584]{1,0:T(8,128)(2,1)S(1)} %copy-done, bf16[1024,3584]{1,0:T(8,128)(2,1)S(1)} %copy-done.1), custom_call_target="tpu_custom_call" | custom-call | flops 939524096 | bytes 14680064 | tf_op jit(solution)/shard_map/up_gate/pallas_call | solution.py:80
  21.3 1.9 %collective-permute-start.3 = (bf16[2,16,1792]{2,1,0:T(8,128)(2,1)S(1)}, bf16[2,16,1792]{2,1,0:T(8,128)(2,1)S(1)}, u32[]{:S(2)}, u32[]{:S(2)}) collective-permute-start(bf16[2,16,1792]{2,1,0:T(8,128)(2,1)S(1)} %add_convert_fusion.4), channel_id=1, source_target_pairs={{0,2},{1,3},{2,0},{3,1},{4,6},{5,7},{6,4},{7,5},{8,10},{9,11},{10,... | collective-permute-start | bytes 344072 | tf_op jit(solution)/shard_map/ppermute | solution.py:22
  23.5 3.9 %collective-permute-done.3 = bf16[2,16,1792]{2,1,0:T(8,128)(2,1)S(1)} collective-permute-done((bf16[2,16,1792]{2,1,0:T(8,128)(2,1)S(1)}, bf16[2,16,1792]{2,1,0:T(8,128)(2,1)S(1)}, u32[]{:S(2)}, u32[]{:S(2)}) %collective-permute-start.3) | collective-permute-done | bytes 114720 | tf_op jit(solution)/shard_map/ppermute | solution.py:22
  27.5 1.9 %collective-permute-done.1 = bf16[2,16,1792]{2,1,0:T(8,128)(2,1)S(1)} collective-permute-done((bf16[2,16,1792]{2,1,0:T(8,128)(2,1)S(1)}, bf16[2,16,1792]{2,1,0:T(8,128)(2,1)S(1)}, u32[]{:S(2)}, u32[]{:S(2)}) %collective-permute-start.1) | collective-permute-done | bytes 114720 | tf_op jit(solution)/shard_map/ppermute | solution.py:22
  29.5 1.8 %collective-permute-start.4 = (bf16[16,3584]{1,0:T(8,128)(2,1)S(1)}, bf16[16,3584]{1,0:T(8,128)(2,1)S(1)}, u32[]{:S(2)}, u32[]{:S(2)}) collective-permute-start(bf16[16,3584]{1,0:T(8,128)(2,1)S(1)} %pad_maximum_fusion.h0), channel_id=1, source_target_pairs={{0,2},{1,3},{2,0},{3,1},{4,6},{5,7},{6,4},{7,5},{8,10},{9,11},{10,... | collective-permute-start | bytes 344072 | tf_op jit(solution)/shard_map/ppermute | solution.py:22
  31.8 1.8 %collective-permute-start.22 = (bf16[2,16,3584]{2,1,0:T(8,128)(2,1)S(1)}, bf16[2,16,3584]{2,1,0:T(8,128)(2,1)S(1)}, u32[]{:S(2)}, u32[]{:S(2)}) collective-permute-start(bf16[2,16,3584]{2,1,0:T(8,128)(2,1)S(1)} %add_convert_fusion), channel_id=1, source_target_pairs={{0,2},{1,3},{2,0},{3,1},{4,6},{5,7},{6,4},{7,5},{8,10},{9,11},{10,... | collective-permute-start | bytes 688136 | tf_op jit(solution)/shard_map/ppermute | solution.py:22
  34.0 11.2 %collective-permute-done.22 = bf16[2,16,3584]{2,1,0:T(8,128)(2,1)S(1)} collective-permute-done((bf16[2,16,3584]{2,1,0:T(8,128)(2,1)S(1)}, bf16[2,16,3584]{2,1,0:T(8,128)(2,1)S(1)}, u32[]{:S(2)}, u32[]{:S(2)}) %collective-permute-start.22) | collective-permute-done | bytes 229408 | tf_op jit(solution)/shard_map/ppermute | solution.py:22
  45.4 2.0 %collective-permute-start.23 = (bf16[16,3584]{1,0:T(8,128)(2,1)S(1)}, bf16[16,3584]{1,0:T(8,128)(2,1)S(1)}, u32[]{:S(2)}, u32[]{:S(2)}) collective-permute-start(bf16[16,3584]{1,0:T(8,128)(2,1)S(1)} %fusion.1.h0), channel_id=1, source_target_pairs={{0,2},{1,3},{2,0},{3,1},{4,6},{5,7},{6,4},{7,5},{8,10},{9,11},{10,... | collective-permute-start | bytes 344072 | tf_op jit(solution)/shard_map/ppermute | solution.py:22
  47.4 2.7 %collective-permute-done.9 = bf16[2,16,3584]{2,1,0:T(8,128)(2,1)S(1)} collective-permute-done((bf16[2,16,3584]{2,1,0:T(8,128)(2,1)S(1)}, bf16[2,16,3584]{2,1,0:T(8,128)(2,1)S(1)}, u32[]{:S(2)}, u32[]{:S(2)}) %collective-permute-start.9) | collective-permute-done | bytes 229408 | tf_op jit(solution)/shard_map/ppermute | solution.py:22
  50.3 1.9 %collective-permute-start.10 = (bf16[16,3584]{1,0:T(8,128)(2,1)S(1)}, bf16[16,3584]{1,0:T(8,128)(2,1)S(1)}, u32[]{:S(2)}, u32[]{:S(2)}) collective-permute-start(bf16[16,3584]{1,0:T(8,128)(2,1)S(1)} %fusion.5.h0), channel_id=1, source_target_pairs={{0,2},{1,3},{2,0},{3,1},{4,6},{5,7},{6,4},{7,5},{8,10},{9,11},{10,... | collective-permute-start | bytes 344072 | tf_op jit(solution)/shard_map/ppermute | solution.py:22
  52.5 1.8 %collective-permute-start.17 = (bf16[16,3584]{1,0:T(8,128)(2,1)S(1)}, bf16[16,3584]{1,0:T(8,128)(2,1)S(1)}, u32[]{:S(2)}, u32[]{:S(2)}) collective-permute-start(bf16[16,3584]{1,0:T(8,128)(2,1)S(1)} %fusion.3.h0), channel_id=1, source_target_pairs={{0,2},{1,3},{2,0},{3,1},{4,6},{5,7},{6,4},{7,5},{8,10},{9,11},{10,... | collective-permute-start | bytes 344072 | tf_op jit(solution)/shard_map/ppermute | solution.py:22
  54.5 0.7 collective-permute-done.10.h2
  55.2 1.1 %down.6 = bf16[64,1024]{1,0:T(8,128)(2,1)S(1)} custom-call(s32[1]{0:T(128)} %bitcast.me_ref, bf16[16,3584]{1,0:T(8,128)(2,1)S(1)} %fusion.1.h0, bf16[16,3584]{1,0:T(8,128)(2,1)S(1)} %collective-permute-done.23.h2, bf16[16,3584]{1,0:T(8,128)(2,1)S(1)} %collective-permute-done.24.h1, bf16[16,3584]{1,0:T(8,128)(2,1)S(1)} %collective-permute-done.25.h3, ...), custom_call_target="tpu_custom_call" | custom-call | flops 469762048 | bytes 7340032 | tf_op jit(solution)/shard_map/down/pallas_call | solution.py:122
  56.3 1.5 %collective-permute-start.26 = (bf16[64,1024]{1,0:T(8,128)(2,1)S(1)}, bf16[64,1024]{1,0:T(8,128)(2,1)S(1)}, u32[]{:S(2)}, u32[]{:S(2)}) collective-permute-start(bf16[64,1024]{1,0:T(8,128)(2,1)S(1)} %down.6), channel_id=1, source_target_pairs={{0,4},{4,0},{8,12},{12,8},{1,5},{5,1},{9,13},{13,9},{2,6},{6,2},{1... | collective-permute-start | bytes 393224 | tf_op jit(solution)/shard_map/ppermute | solution.py:22
  58.9 1.3 %down.5 = bf16[64,1024]{1,0:T(8,128)(2,1)S(1)} custom-call(s32[1]{0:T(128)} %bitcast.me_ref, bf16[16,3584]{1,0:T(8,128)(2,1)S(1)} %fusion.5.h0, bf16[16,3584]{1,0:T(8,128)(2,1)S(1)} %collective-permute-done.10.h2, bf16[16,3584]{1,0:T(8,128)(2,1)S(1)} %collective-permute-done.11.h1, bf16[16,3584]{1,0:T(8,128)(2,1)S(1)} %collective-permute-done.12.h3, ...), custom_call_target="tpu_custom_call" | custom-call | flops 469762048 | bytes 7340032 | tf_op jit(solution)/shard_map/down/pallas_call | solution.py:122
  60.2 1.1 %collective-permute-start.13 = (bf16[64,1024]{1,0:T(8,128)(2,1)S(1)}, bf16[64,1024]{1,0:T(8,128)(2,1)S(1)}, u32[]{:S(2)}, u32[]{:S(2)}) collective-permute-start(bf16[64,1024]{1,0:T(8,128)(2,1)S(1)} %down.5), channel_id=1, source_target_pairs={{0,4},{4,0},{8,12},{12,8},{1,5},{5,1},{9,13},{13,9},{2,6},{6,2},{1... | collective-permute-start | bytes 393224 | tf_op jit(solution)/shard_map/ppermute | solution.py:22
  61.3 1.0 %collective-permute-done.26.refs_0_ = bf16[64,1024]{1,0:T(8,128)(2,1)S(1)} collective-permute-done((bf16[64,1024]{1,0:T(8,128)(2,1)S(1)}, bf16[64,1024]{1,0:T(8,128)(2,1)S(1)}, u32[]{:S(2)}, u32[]{:S(2)}) %collective-permute-start.26) | collective-permute-done | bytes 131104 | tf_op jit(solution)/shard_map/ppermute | solution.py:22
  62.3 1.1 %down.7 = bf16[64,1024]{1,0:T(8,128)(2,1)S(1)} custom-call(s32[1]{0:T(128)} %bitcast.me_ref, bf16[16,3584]{1,0:T(8,128)(2,1)S(1)} %fusion.3.h0, bf16[16,3584]{1,0:T(8,128)(2,1)S(1)} %collective-permute-done.17.h2, bf16[16,3584]{1,0:T(8,128)(2,1)S(1)} %collective-permute-done.18.h1, bf16[16,3584]{1,0:T(8,128)(2,1)S(1)} %collective-permute-done.19.h3, ...), custom_call_target="tpu_custom_call" | custom-call | flops 469762048 | bytes 7340032 | tf_op jit(solution)/shard_map/down/pallas_call | solution.py:122
  63.4 2.4 %collective-permute-start.27 = (bf16[64,1024]{1,0:T(8,128)(2,1)S(1)}, bf16[64,1024]{1,0:T(8,128)(2,1)S(1)}, u32[]{:S(2)}, u32[]{:S(2)}) collective-permute-start(bf16[64,1024]{1,0:T(8,128)(2,1)S(1)} %down.7), channel_id=1, source_target_pairs={{0,8},{4,12},{8,0},{12,4},{1,9},{5,13},{9,1},{13,5},{2,10},{6,14},... | collective-permute-start | bytes 393224 | tf_op jit(solution)/shard_map/ppermute | solution.py:22
  65.8 1.1 %down.4 = f32[64,1024]{1,0:T(8,128)S(1)} custom-call(s32[1]{0:T(128)} %bitcast.me_ref, bf16[16,3584]{1,0:T(8,128)(2,1)S(1)} %pad_maximum_fusion.h0, bf16[16,3584]{1,0:T(8,128)(2,1)S(1)} %collective-permute-done.4.h2, bf16[16,3584]{1,0:T(8,128)(2,1)S(1)} %collective-permute-done.5.h1, bf16[16,3584]{1,0:T(8,128)(2,1)S(1)} %collective-permute-done.6.h3, ...), custom_call_target="tpu_custom_call" | custom-call | flops 469762048 | bytes 7340032 | tf_op jit(solution)/shard_map/down/pallas_call | solution.py:122
  66.9 5.3 %collective-permute-done.27 = bf16[64,1024]{1,0:T(8,128)(2,1)S(1)} collective-permute-done((bf16[64,1024]{1,0:T(8,128)(2,1)S(1)}, bf16[64,1024]{1,0:T(8,128)(2,1)S(1)}, u32[]{:S(2)}, u32[]{:S(2)}) %collective-permute-start.27) | collective-permute-done | bytes 131104 | tf_op jit(solution)/shard_map/ppermute | solution.py:22
  72.2 0.7 add_convert_fusion.3
  (60 shorter events, 4.7 us)
Async XLA Ops:
  0.0 14.3 %collective-permute-start.14 = (bf16[64,1024]{1,0:T(8,128)(2,1)}, bf16[64,1024]{1,0:T(8,128)(2,1)S(1)}, u32[]{:S(2)}, u32[]{:S(2)}) collective-permute-start(bf16[64,1024]{1,0:T(8,128)(2,1)} %refs_0_.1), channel_id=1, source_target_pairs={{0,8},{4,12},{8,0},{12,4},{1,9},{5,13},{9,1},{13,5},{2,10},{6,14},... | collective-permute-start | bytes 393224 | tf_op jit(solution)/shard_map/ppermute | solution.py:22
  4.1 12.4 %collective-permute-start.20 = (bf16[64,1024]{1,0:T(8,128)(2,1)}, bf16[64,1024]{1,0:T(8,128)(2,1)S(1)}, u32[]{:S(2)}, u32[]{:S(2)}) collective-permute-start(bf16[64,1024]{1,0:T(8,128)(2,1)} %refs_0_.1), channel_id=1, source_target_pairs={{0,12},{4,8},{8,4},{12,0},{1,13},{5,9},{9,5},{13,1},{2,14},{6,10},... | collective-permute-start | bytes 393224 | tf_op jit(solution)/shard_map/ppermute | solution.py:22
  5.4 13.7 %collective-permute-start.7 = (bf16[64,1024]{1,0:T(8,128)(2,1)}, bf16[64,1024]{1,0:T(8,128)(2,1)S(1)}, u32[]{:S(2)}, u32[]{:S(2)}) collective-permute-start(bf16[64,1024]{1,0:T(8,128)(2,1)} %refs_0_.1), channel_id=1, source_target_pairs={{0,4},{4,0},{8,12},{12,8},{1,5},{5,1},{9,13},{13,9},{2,6},{6,2},{1... | collective-permute-start | bytes 393224 | tf_op jit(solution)/shard_map/ppermute | solution.py:22
  5.6 3.1 %copy-start = (bf16[1024,3584]{1,0:T(8,128)(2,1)S(1)}, bf16[1024,3584]{1,0:T(8,128)(2,1)}, u32[]{:S(2)}) copy-start(bf16[1024,3584]{1,0:T(8,128)(2,1)} %refs_1_.9) | copy-start | bytes 22020100
  5.6 5.2 %copy-start.1 = (bf16[1024,3584]{1,0:T(8,128)(2,1)S(1)}, bf16[1024,3584]{1,0:T(8,128)(2,1)}, u32[]{:S(2)}) copy-start(bf16[1024,3584]{1,0:T(8,128)(2,1)} %refs_2_.9) | copy-start | bytes 22020100
  12.0 9.3 %collective-permute-start.2 = (bf16[2,32,1792]{2,1,0:T(8,128)(2,1)S(1)}, bf16[2,32,1792]{2,1,0:T(8,128)(2,1)S(1)}, u32[]{:S(2)}, u32[]{:S(2)}) collective-permute-start(bf16[2,32,1792]{2,1,0:T(8,128)(2,1)S(1)} %get-tuple-element.18), channel_id=1, source_target_pairs={{0,1},{1,0},{2,3},{3,2},{4,5},{5,4},{6,7},{7,6},{8,9},{9,8},{10,11... | collective-permute-start | bytes 688136 | tf_op jit(solution)/shard_map/ppermute | solution.py:22
  13.2 10.0 %collective-permute-start = (bf16[2,32,1792]{2,1,0:T(8,128)(2,1)S(1)}, bf16[2,32,1792]{2,1,0:T(8,128)(2,1)S(1)}, u32[]{:S(2)}, u32[]{:S(2)}) collective-permute-start(bf16[2,32,1792]{2,1,0:T(8,128)(2,1)S(1)} %get-tuple-element.16), channel_id=1, source_target_pairs={{0,1},{1,0},{2,3},{3,2},{4,5},{5,4},{6,7},{7,6},{8,9},{9,8},{10,11... | collective-permute-start | bytes 688136 | tf_op jit(solution)/shard_map/ppermute | solution.py:22
  16.4 15.0 %collective-permute-start.15 = (bf16[2,32,3584]{2,1,0:T(8,128)(2,1)S(1)}, bf16[2,32,3584]{2,1,0:T(8,128)(2,1)S(1)}, u32[]{:S(2)}, u32[]{:S(2)}) collective-permute-start(bf16[2,32,3584]{2,1,0:T(8,128)(2,1)S(1)} %get-tuple-element.22), channel_id=1, source_target_pairs={{0,1},{1,0},{2,3},{3,2},{4,5},{5,4},{6,7},{7,6},{8,9},{9,8},{10,11... | collective-permute-start | bytes 1376264 | tf_op jit(solution)/shard_map/ppermute | solution.py:22
  18.5 36.6 %slice-start = ((s8[7340032]{0:T(1024)(128)(4,1)}), s8[4194304]{0:T(1024)(128)(4,1)S(1)}, s32[]{:S(2)}) async-start(s8[7340032]{0:T(1024)(128)(4,1)} %bitcast.51), calls=%async_computation | async-start | bytes 8388608
  18.6 36.6 %slice-start.1 = ((s8[7340032]{0:T(1024)(128)(4,1)}), s8[3145728]{0:T(1024)(128)(4,1)S(1)}, s32[]{:S(2)}) async-start(s8[7340032]{0:T(1024)(128)(4,1)} %bitcast.51), calls=%async_computation.1 | async-start | bytes 6291456
  18.6 13.2 %collective-permute-start.21 = (bf16[2,32,3584]{2,1,0:T(8,128)(2,1)S(1)}, bf16[2,32,3584]{2,1,0:T(8,128)(2,1)S(1)}, u32[]{:S(2)}, u32[]{:S(2)}) collective-permute-start(bf16[2,32,3584]{2,1,0:T(8,128)(2,1)S(1)} %get-tuple-element.24), channel_id=1, source_target_pairs={{0,1},{1,0},{2,3},{3,2},{4,5},{5,4},{6,7},{7,6},{8,9},{9,8},{10,11... | collective-permute-start | bytes 1376264 | tf_op jit(solution)/shard_map/ppermute | solution.py:22
  21.2 12.4 %collective-permute-start.8 = (bf16[2,32,3584]{2,1,0:T(8,128)(2,1)S(1)}, bf16[2,32,3584]{2,1,0:T(8,128)(2,1)S(1)}, u32[]{:S(2)}, u32[]{:S(2)}) collective-permute-start(bf16[2,32,3584]{2,1,0:T(8,128)(2,1)S(1)} %get-tuple-element.20), channel_id=1, source_target_pairs={{0,1},{1,0},{2,3},{3,2},{4,5},{5,4},{6,7},{7,6},{8,9},{9,8},{10,11... | collective-permute-start | bytes 1376264 | tf_op jit(solution)/shard_map/ppermute | solution.py:22
  21.3 6.1 %collective-permute-start.3 = (bf16[2,16,1792]{2,1,0:T(8,128)(2,1)S(1)}, bf16[2,16,1792]{2,1,0:T(8,128)(2,1)S(1)}, u32[]{:S(2)}, u32[]{:S(2)}) collective-permute-start(bf16[2,16,1792]{2,1,0:T(8,128)(2,1)S(1)} %add_convert_fusion.4), channel_id=1, source_target_pairs={{0,2},{1,3},{2,0},{3,1},{4,6},{5,7},{6,4},{7,5},{8,10},{9,11},{10,... | collective-permute-start | bytes 344072 | tf_op jit(solution)/shard_map/ppermute | solution.py:22
  23.2 6.2 %collective-permute-start.1 = (bf16[2,16,1792]{2,1,0:T(8,128)(2,1)S(1)}, bf16[2,16,1792]{2,1,0:T(8,128)(2,1)S(1)}, u32[]{:S(2)}, u32[]{:S(2)}) collective-permute-start(bf16[2,16,1792]{2,1,0:T(8,128)(2,1)S(1)} %add_convert_fusion.5), channel_id=1, source_target_pairs={{0,2},{1,3},{2,0},{3,1},{4,6},{5,7},{6,4},{7,5},{8,10},{9,11},{10,... | collective-permute-start | bytes 344072 | tf_op jit(solution)/shard_map/ppermute | solution.py:22
  29.5 28.3 %collective-permute-start.4 = (bf16[16,3584]{1,0:T(8,128)(2,1)S(1)}, bf16[16,3584]{1,0:T(8,128)(2,1)S(1)}, u32[]{:S(2)}, u32[]{:S(2)}) collective-permute-start(bf16[16,3584]{1,0:T(8,128)(2,1)S(1)} %pad_maximum_fusion.h0), channel_id=1, source_target_pairs={{0,2},{1,3},{2,0},{3,1},{4,6},{5,7},{6,4},{7,5},{8,10},{9,11},{10,... | collective-permute-start | bytes 344072 | tf_op jit(solution)/shard_map/ppermute | solution.py:22
  31.4 20.8 %collective-permute-start.16 = (bf16[2,16,3584]{2,1,0:T(8,128)(2,1)S(1)}, bf16[2,16,3584]{2,1,0:T(8,128)(2,1)S(1)}, u32[]{:S(2)}, u32[]{:S(2)}) collective-permute-start(bf16[2,16,3584]{2,1,0:T(8,128)(2,1)S(1)} %add_convert_fusion.1), channel_id=1, source_target_pairs={{0,2},{1,3},{2,0},{3,1},{4,6},{5,7},{6,4},{7,5},{8,10},{9,11},{10,... | collective-permute-start | bytes 688136 | tf_op jit(solution)/shard_map/ppermute | solution.py:22
  31.8 13.4 %collective-permute-start.22 = (bf16[2,16,3584]{2,1,0:T(8,128)(2,1)S(1)}, bf16[2,16,3584]{2,1,0:T(8,128)(2,1)S(1)}, u32[]{:S(2)}, u32[]{:S(2)}) collective-permute-start(bf16[2,16,3584]{2,1,0:T(8,128)(2,1)S(1)} %add_convert_fusion), channel_id=1, source_target_pairs={{0,2},{1,3},{2,0},{3,1},{4,6},{5,7},{6,4},{7,5},{8,10},{9,11},{10,... | collective-permute-start | bytes 688136 | tf_op jit(solution)/shard_map/ppermute | solution.py:22
  33.7 16.5 %collective-permute-start.9 = (bf16[2,16,3584]{2,1,0:T(8,128)(2,1)S(1)}, bf16[2,16,3584]{2,1,0:T(8,128)(2,1)S(1)}, u32[]{:S(2)}, u32[]{:S(2)}) collective-permute-start(bf16[2,16,3584]{2,1,0:T(8,128)(2,1)S(1)} %add_convert_fusion.2), channel_id=1, source_target_pairs={{0,2},{1,3},{2,0},{3,1},{4,6},{5,7},{6,4},{7,5},{8,10},{9,11},{10,... | collective-permute-start | bytes 688136 | tf_op jit(solution)/shard_map/ppermute | solution.py:22
  45.4 6.9 %collective-permute-start.23 = (bf16[16,3584]{1,0:T(8,128)(2,1)S(1)}, bf16[16,3584]{1,0:T(8,128)(2,1)S(1)}, u32[]{:S(2)}, u32[]{:S(2)}) collective-permute-start(bf16[16,3584]{1,0:T(8,128)(2,1)S(1)} %fusion.1.h0), channel_id=1, source_target_pairs={{0,2},{1,3},{2,0},{3,1},{4,6},{5,7},{6,4},{7,5},{8,10},{9,11},{10,... | collective-permute-start | bytes 344072 | tf_op jit(solution)/shard_map/ppermute | solution.py:22
  47.4 6.8 %collective-permute-start.24 = (bf16[16,3584]{1,0:T(8,128)(2,1)S(1)}, bf16[16,3584]{1,0:T(8,128)(2,1)S(1)}, u32[]{:S(2)}, u32[]{:S(2)}) collective-permute-start(bf16[16,3584]{1,0:T(8,128)(2,1)S(1)} %fusion.1.h0), channel_id=1, source_target_pairs={{0,1},{1,0},{2,3},{3,2},{4,5},{5,4},{6,7},{7,6},{8,9},{9,8},{10,11... | collective-permute-start | bytes 344072 | tf_op jit(solution)/shard_map/ppermute | solution.py:22
  50.3 4.9 %collective-permute-start.10 = (bf16[16,3584]{1,0:T(8,128)(2,1)S(1)}, bf16[16,3584]{1,0:T(8,128)(2,1)S(1)}, u32[]{:S(2)}, u32[]{:S(2)}) collective-permute-start(bf16[16,3584]{1,0:T(8,128)(2,1)S(1)} %fusion.5.h0), channel_id=1, source_target_pairs={{0,2},{1,3},{2,0},{3,1},{4,6},{5,7},{6,4},{7,5},{8,10},{9,11},{10,... | collective-permute-start | bytes 344072 | tf_op jit(solution)/shard_map/ppermute | solution.py:22
  52.3 2.9 %collective-permute-start.25 = (bf16[16,3584]{1,0:T(8,128)(2,1)S(1)}, bf16[16,3584]{1,0:T(8,128)(2,1)S(1)}, u32[]{:S(2)}, u32[]{:S(2)}) collective-permute-start(bf16[16,3584]{1,0:T(8,128)(2,1)S(1)} %collective-permute-done.23.h2), channel_id=1, source_target_pairs={{0,1},{1,0},{2,3},{3,2},{4,5},{5,4},{6,7},{7,6},{8,9},{9,8},{10,11... | collective-permute-start | bytes 344072 | tf_op jit(solution)/shard_map/ppermute | solution.py:22
  52.5 5.6 %collective-permute-start.17 = (bf16[16,3584]{1,0:T(8,128)(2,1)S(1)}, bf16[16,3584]{1,0:T(8,128)(2,1)S(1)}, u32[]{:S(2)}, u32[]{:S(2)}) collective-permute-start(bf16[16,3584]{1,0:T(8,128)(2,1)S(1)} %fusion.3.h0), channel_id=1, source_target_pairs={{0,2},{1,3},{2,0},{3,1},{4,6},{5,7},{6,4},{7,5},{8,10},{9,11},{10,... | collective-permute-start | bytes 344072 | tf_op jit(solution)/shard_map/ppermute | solution.py:22
  54.3 4.1 %collective-permute-start.11 = (bf16[16,3584]{1,0:T(8,128)(2,1)S(1)}, bf16[16,3584]{1,0:T(8,128)(2,1)S(1)}, u32[]{:S(2)}, u32[]{:S(2)}) collective-permute-start(bf16[16,3584]{1,0:T(8,128)(2,1)S(1)} %fusion.5.h0), channel_id=1, source_target_pairs={{0,1},{1,0},{2,3},{3,2},{4,5},{5,4},{6,7},{7,6},{8,9},{9,8},{10,11... | collective-permute-start | bytes 344072 | tf_op jit(solution)/shard_map/ppermute | solution.py:22
  55.1 3.4 %collective-permute-start.12 = (bf16[16,3584]{1,0:T(8,128)(2,1)S(1)}, bf16[16,3584]{1,0:T(8,128)(2,1)S(1)}, u32[]{:S(2)}, u32[]{:S(2)}) collective-permute-start(bf16[16,3584]{1,0:T(8,128)(2,1)S(1)} %collective-permute-done.10.h2), channel_id=1, source_target_pairs={{0,1},{1,0},{2,3},{3,2},{4,5},{5,4},{6,7},{7,6},{8,9},{9,8},{10,11... | collective-permute-start | bytes 344072 | tf_op jit(solution)/shard_map/ppermute | solution.py:22
  56.3 6.0 %collective-permute-start.26 = (bf16[64,1024]{1,0:T(8,128)(2,1)S(1)}, bf16[64,1024]{1,0:T(8,128)(2,1)S(1)}, u32[]{:S(2)}, u32[]{:S(2)}) collective-permute-start(bf16[64,1024]{1,0:T(8,128)(2,1)S(1)} %down.6), channel_id=1, source_target_pairs={{0,4},{4,0},{8,12},{12,8},{1,5},{5,1},{9,13},{13,9},{2,6},{6,2},{1... | collective-permute-start | bytes 393224 | tf_op jit(solution)/shard_map/ppermute | solution.py:22
  57.8 2.4 %collective-permute-start.18 = (bf16[16,3584]{1,0:T(8,128)(2,1)S(1)}, bf16[16,3584]{1,0:T(8,128)(2,1)S(1)}, u32[]{:S(2)}, u32[]{:S(2)}) collective-permute-start(bf16[16,3584]{1,0:T(8,128)(2,1)S(1)} %fusion.3.h0), channel_id=1, source_target_pairs={{0,1},{1,0},{2,3},{3,2},{4,5},{5,4},{6,7},{7,6},{8,9},{9,8},{10,11... | collective-permute-start | bytes 344072 | tf_op jit(solution)/shard_map/ppermute | solution.py:22
  58.1 3.2 %collective-permute-start.19 = (bf16[16,3584]{1,0:T(8,128)(2,1)S(1)}, bf16[16,3584]{1,0:T(8,128)(2,1)S(1)}, u32[]{:S(2)}, u32[]{:S(2)}) collective-permute-start(bf16[16,3584]{1,0:T(8,128)(2,1)S(1)} %collective-permute-done.17.h2), channel_id=1, source_target_pairs={{0,1},{1,0},{2,3},{3,2},{4,5},{5,4},{6,7},{7,6},{8,9},{9,8},{10,11... | collective-permute-start | bytes 344072 | tf_op jit(solution)/shard_map/ppermute | solution.py:22
  58.3 7.5 %collective-permute-start.5 = (bf16[16,3584]{1,0:T(8,128)(2,1)S(1)}, bf16[16,3584]{1,0:T(8,128)(2,1)S(1)}, u32[]{:S(2)}, u32[]{:S(2)}) collective-permute-start(bf16[16,3584]{1,0:T(8,128)(2,1)S(1)} %pad_maximum_fusion.h0), channel_id=1, source_target_pairs={{0,1},{1,0},{2,3},{3,2},{4,5},{5,4},{6,7},{7,6},{8,9},{9,8},{10,11... | collective-permute-start | bytes 344072 | tf_op jit(solution)/shard_map/ppermute | solution.py:22
  58.6 7.2 %collective-permute-start.6 = (bf16[16,3584]{1,0:T(8,128)(2,1)S(1)}, bf16[16,3584]{1,0:T(8,128)(2,1)S(1)}, u32[]{:S(2)}, u32[]{:S(2)}) collective-permute-start(bf16[16,3584]{1,0:T(8,128)(2,1)S(1)} %collective-permute-done.4.h2), channel_id=1, source_target_pairs={{0,1},{1,0},{2,3},{3,2},{4,5},{5,4},{6,7},{7,6},{8,9},{9,8},{10,11... | collective-permute-start | bytes 344072 | tf_op jit(solution)/shard_map/ppermute | solution.py:22
  60.2 6.7 %collective-permute-start.13 = (bf16[64,1024]{1,0:T(8,128)(2,1)S(1)}, bf16[64,1024]{1,0:T(8,128)(2,1)S(1)}, u32[]{:S(2)}, u32[]{:S(2)}) collective-permute-start(bf16[64,1024]{1,0:T(8,128)(2,1)S(1)} %down.5), channel_id=1, source_target_pairs={{0,4},{4,0},{8,12},{12,8},{1,5},{5,1},{9,13},{13,9},{2,6},{6,2},{1... | collective-permute-start | bytes 393224 | tf_op jit(solution)/shard_map/ppermute | solution.py:22
  63.4 8.8 %collective-permute-start.27 = (bf16[64,1024]{1,0:T(8,128)(2,1)S(1)}, bf16[64,1024]{1,0:T(8,128)(2,1)S(1)}, u32[]{:S(2)}, u32[]{:S(2)}) collective-permute-start(bf16[64,1024]{1,0:T(8,128)(2,1)S(1)} %down.7), channel_id=1, source_target_pairs={{0,8},{4,12},{8,0},{12,4},{1,9},{5,13},{9,1},{13,5},{2,10},{6,14},... | collective-permute-start | bytes 393224 | tf_op jit(solution)/shard_map/ppermute | solution.py:22
